TPU v7x, 16 devices: a whole 2x2x2 slice. The times are simulated.
16 devices in a mesh: rep: 1, dp: 16 (over x, y, z, core).
Axes of the slice: x: 2, y: 2, z: 2, core: 2. Of those that a mesh axis runs over, the one named last changes fastest.
Arguments:
- x: bfloat16 [16, 2048, 1024], P(('rep', 'dp'))
- dy: bfloat16 [16, 2048, 1024], P(('rep', 'dp'))
- w_gate: bfloat16 [2, 1024, 2816], replicated
- w_up: bfloat16 [2, 1024, 2816], replicated
- w_down: bfloat16 [2, 2816, 1024], replicated
- m_w_gate: float32 [2, 1024, 2816], P(None, 'dp')
- m_w_up: float32 [2, 1024, 2816], P(None, 'dp')
- m_w_down: float32 [2, 2816, 1024], P(None, 'dp')
- v_w_gate: float32 [2, 1024, 2816], P(None, 'dp')
- v_w_up: float32 [2, 1024, 2816], P(None, 'dp')
- v_w_down: float32 [2, 2816, 1024], P(None, 'dp')
Outputs:
- output 1: bfloat16 [2, 1024, 2816], P('rep')
- output 2: bfloat16 [2, 1024, 2816], P('rep')
- output 3: bfloat16 [2, 2816, 1024], P('rep')
- output 4: float32 [2, 1024, 2816], P('rep', 'dp')
- output 5: float32 [2, 1024, 2816], P('rep', 'dp')
- output 6: float32 [2, 2816, 1024], P('rep', 'dp')
- output 7: float32 [2, 1024, 2816], P('rep', 'dp')
- output 8: float32 [2, 1024, 2816], P('rep', 'dp')
- output 9: float32 [2, 2816, 1024], P('rep', 'dp')
All inputs are finite; a program needn't handle non-finite values.
Results may differ from a plain program's by a relative error of at most 0.022.
Values are sent between devices in bfloat16 or wider.
A program may use at most 2 GiB of HBM per device.

v0:
```python
import jax
import jax.numpy as jnp
from jax import lax

NAMES = ("w_gate", "w_up", "w_down")


def matmul(a, w):
    return jnp.dot(a, w, preferred_element_type=jnp.float32).astype(jnp.bfloat16)


def normed(h):
    wide = h.astype(jnp.float32)
    scale = lax.rsqrt(jnp.mean(wide**2, -1, keepdims=True) + 1e-6)
    return (wide * scale).astype(jnp.bfloat16)


def layer(h, w):
    a = normed(h)
    gate = jnp.dot(a, w["w_gate"], preferred_element_type=jnp.float32)
    up = jnp.dot(a, w["w_up"], preferred_element_type=jnp.float32)
    return h + matmul((jax.nn.silu(gate) * up).astype(jnp.bfloat16), w["w_down"])


def adamw(w, m, v, g):
    m = 0.9 * m + 0.1 * g
    v = 0.95 * v + 0.05 * g * g
    step = m * lax.rsqrt(v + 1e-8) + 0.1 * w
    return (w - 0.02 * step).astype(jnp.bfloat16), m, v


def clipped(gradients, sum_of_squares, count):
    factor = jnp.minimum(1.0, 0.5 * lax.rsqrt(sum_of_squares / count + 1e-30))
    return [g * factor for g in gradients]


def stack(weights, h):
    for number in range(weights["w_gate"].shape[0]):
        h = layer(h, {name: w[number] for name, w in weights.items()})
    return h


def solution(mesh):
    groups = mesh.shape["rep"]

    def step(x, dy, *arrays):
        weights, m, v = (arrays[i : i + 3] for i in (0, 3, 6))
        x, dy = (t.reshape(groups, -1, *t.shape[1:]) for t in (x, dy))

        def of_a_group(x, dy):
            _, back = jax.vjp(lambda w: stack(w, x), dict(zip(NAMES, weights, strict=True)))
            by_weights = back(dy)[0]
            gradients = [by_weights[name].astype(jnp.float32) for name in NAMES]
            gradients = clipped(gradients, sum(jnp.sum(g * g) for g in gradients), sum(g.size for g in gradients))
            new = [adamw(w.astype(jnp.float32), m, v, g) for w, m, v, g in zip(weights, m, v, gradients, strict=True)]
            return tuple(one[which] for which in range(3) for one in new)

        return tuple(t.reshape(-1, *t.shape[2:]) for t in jax.vmap(of_a_group)(x, dy))

    return step
```

profile of v0, /device:TPU:0, one launch (start us, length us, event | category | flops | bytes accessed | tf_op | source)
XLA Modules:
  0.0 1553.6 jit_solution(1047542634879374569)
XLA Ops:
  18.3 19.6 %fusion.173 = f32[2048,2816]{1,0:T(8,128)} fusion(bf16[2,1024,2816]{2,1,0:T(8,128)(2,1)} %param.12, bf16[1,2048,1024]{1,2,0:T(8,128)(2,1)S(1)} %fusion.157), kind=kOutput, calls=%fused_computation.224 | convolution fusion | flops 11811160064 | bytes 33030144 | tf_op jit(solution)/vmap(jvp())/dot_general | solution.py:20
  37.9 26.6 %fusion.150 = (bf16[1,2048,2816]{2,1,0:T(8,128)(2,1)}, f32[2048,2816]{1,0:T(8,128)}) fusion(f32[2048,2816]{1,0:T(8,128)} %fusion.173, bf16[2,1024,2816]{2,1,0:T(8,128)(2,1)} %param.17, bf16[1,2048,1024]{1,2,0:T(8,128)(2,1)S(1)} %fusion.157), kind=kOutput, calls=%fused_computation.189 | convolution fusion | flops 11845763072 | bytes 67633152 | tf_op jit(solution)/vmap(jvp())/dot_general | solution.py:21
  64.5 19.5 %fusion.160 = (f32[2048]{0:T(1024)S(1)}, bf16[1,2048,1024]{1,2,0:T(8,128)(2,1)}) fusion(bf16[1,2048,1024]{1,2,0:T(8,128)(2,1)} %copy.1, bf16[2,2816,1024]{2,1,0:T(8,128)(2,1)} %param.15, bf16[1,2048,2816]{2,1,0:T(8,128)(2,1)} %get-tuple-element.263), kind=kOutput, calls=%fused_computation.211 | convolution fusion | flops 11821643776 | bytes 25698304 | tf_op jit(solution)/vmap(jvp())/dot_general | solution.py:9
  87.9 19.6 %fusion.163 = f32[2048,2816]{1,0:T(8,128)} fusion(bf16[2,1024,2816]{2,1,0:T(8,128)(2,1)} %param.12, bf16[1,2048,1024]{1,2,0:T(8,128)(2,1)S(1)} %fusion.161), kind=kOutput, calls=%fused_computation.214 | convolution fusion | flops 11811160064 | bytes 33030144 | tf_op jit(solution)/vmap(jvp())/dot_general | solution.py:20
  107.5 26.8 %fusion.149 = (bf16[1,2048,2816]{2,1,0:T(8,128)(2,1)}, f32[2048,2816]{1,0:T(8,128)}) fusion(f32[2048,2816]{1,0:T(8,128)} %fusion.163, bf16[2,1024,2816]{2,1,0:T(8,128)(2,1)} %param.17, bf16[1,2048,1024]{1,2,0:T(8,128)(2,1)S(1)} %fusion.161), kind=kOutput, calls=%fused_computation.187 | convolution fusion | flops 11845763072 | bytes 67633152 | tf_op jit(solution)/vmap(jvp())/dot_general | solution.py:21
  134.3 15.3 copy.3
  149.7 152.0 %while.16 = (bf16[1,2048,2816]{1,2,0:T(8,128)(2,1)}, bf16[1,2048,1024]{2,1,0:T(8,128)(2,1)}, f32[176,1024]{1,0:T(8,128)S(1)}, f32[176,1024]{1,0:T(8,128)}, u32[]...) while((bf16[1,2048,2816]{1,2,0:T(8,128)(2,1)}, ...), condition=%wide.windowed_dot_general_cond_rs.4.clone, body=%wide.windowed_dot_general_body_rs.4.clone.sunk | while | flops 2959638528 | bytes 57410128 | solution.py:9
  164.4 14.5 collective-permute-start.18
  207.1 8.6 collective-permute-start.18
  226.7 9.7 collective-permute-start.16
  246.3 7.9 collective-permute-start.18
  265.2 9.7 collective-permute-start.16
  301.7 9.6 collective-permute-start.28
  317.8 15.2 copy.5
  333.1 34.1 %convert_multiply_fusion.2 = (bf16[1,2048,2816]{2,1,0:T(8,128)(2,1)}, bf16[1,2048,2816]{2,1,0:T(8,128)(2,1)}) fusion(f32[2048,2816]{1,0:T(8,128)} %fusion.163, f32[2048,2816]{1,0:T(8,128)} %get-tuple-element.270, bf16[2,2816,1024]{2,1,0:T(8,128)(2,1)} %param.15, bf16[1,2048,1024]{2,1,0:T(8,128)(2,1)} %get-tuple-element.744), kind=kOutput, calls=%fused_computation.170 | convolution fusion | flops 11903434752 | bytes 79167488 | tf_op jit(solution)/vmap(transpose(jvp()))/dot_general | solution.py:9
  367.1 18.1 %fusion.142 = bf16[2048,1024]{0,1:T(8,128)(2,1)} fusion(bf16[1,2048,2816]{2,1,0:T(8,128)(2,1)} %get-tuple-element.541, bf16[2,1024,2816]{2,1,0:T(8,128)(2,1)} %param.12), kind=kOutput, calls=%fused_computation.176 | convolution fusion | flops 11811160064 | bytes 21495808 | tf_op jit(solution)/vmap(transpose(jvp()))/dot_general | solution.py:20
  385.3 19.0 %fusion.162 = (f32[2048]{0:T(1024)S(1)}, bf16[2048,1024]{0,1:T(8,128)(2,1)}) fusion(bf16[1,2048,1024]{1,2,0:T(8,128)(2,1)S(1)} %copy-done.14, bf16[2048,1024]{0,1:T(8,128)(2,1)} %fusion.142, bf16[2,1024,2816]{2,1,0:T(8,128)(2,1)} %param.17, bf16[1,2048,2816]{2,1,0:T(8,128)(2,1)} %get-tuple-element.613), kind=kOutput, calls=%fused_computation.213 | convolution fusion | flops 11821643776 | bytes 29892608 | tf_op jit(solution)/vmap(transpose(jvp()))/dot_general | solution.py:21
  417.6 149.4 %while.17 = (bf16[1,2048,1024]{2,1,0:T(8,128)(2,1)}, bf16[1,2048,2816]{1,2,0:T(8,128)(2,1)}, f32[1024,176]{0,1:T(8,128)S(1)}, f32[1024,176]{0,1:T(8,128)}, u32[]...) while((bf16[1,2048,1024]{2,1,0:T(8,128)(2,1)}, ...), condition=%wide.windowed_dot_general_cond_rs.5.clone, body=%wide.windowed_dot_general_body_rs.5.clone.sunk | while | flops 2959638528 | bytes 57410128 | solution.py:9
  431.2 14.6 collective-permute-start.22
  491.9 9.7 collective-permute-start.20
  529.6 9.7 collective-permute-start.20
  549.2 7.9 collective-permute-start.22
  567.0 9.6 collective-permute-start.29
  576.6 160.5 %while.14 = (bf16[1,2048,2816]{2,1,0:T(8,128)(2,1)}, bf16[1,2048,1024]{1,2,0:T(8,128)(2,1)}, f32[2816,64]{0,1:T(8,128)}, f32[2816,64]{0,1:T(8,128)}, u32[]{:T(12...) while((bf16[1,2048,2816]{2,1,0:T(8,128)(2,1)}, ...), condition=%wide.windowed_dot_general_cond_rs.2.clone, body=%wide.windowed_dot_general_body_rs.2.clone.sunk | while | flops 2955968512 | bytes 108790456 | solution.py:21
  592.3 14.6 collective-permute-start.10
  658.4 8.9 collective-permute-start.8
  737.1 9.5 collective-permute-start.26
  746.6 34.1 %convert_multiply_fusion = (bf16[1,2048,2816]{2,1,0:T(8,128)(2,1)}, bf16[1,2048,2816]{2,1,0:T(8,128)(2,1)}) fusion(f32[2048,2816]{1,0:T(8,128)} %fusion.173, f32[2048,2816]{1,0:T(8,128)} %get-tuple-element.264, bf16[2,2816,1024]{2,1,0:T(8,128)(2,1)} %param.15, bf16[1,2048,1024]{1,2,0:T(8,128)(2,1)} %fusion.185), kind=kOutput, calls=%fused_computation.168 | convolution fusion | flops 11903434752 | bytes 79167488 | tf_op jit(solution)/vmap(transpose(jvp()))/dot_general | solution.py:9
  780.7 159.9 %while.15 = (bf16[1,2048,2816]{2,1,0:T(8,128)(2,1)}, bf16[1,2048,1024]{1,2,0:T(8,128)(2,1)}, f32[2816,64]{0,1:T(8,128)}, f32[2816,64]{0,1:T(8,128)}, u32[]{:T(12...) while((bf16[1,2048,2816]{2,1,0:T(8,128)(2,1)}, ...), condition=%wide.windowed_dot_general_cond_rs.3.clone, body=%wide.windowed_dot_general_body_rs.3.clone.sunk | while | flops 2955968512 | bytes 108790456 | solution.py:21
  796.4 14.6 collective-permute-start.14
  901.7 8.9 collective-permute-start.12
  940.6 160.7 %while.12 = (bf16[1,2048,2816]{2,1,0:T(8,128)(2,1)}, bf16[1,2048,1024]{1,2,0:T(8,128)(2,1)}, f32[2816,64]{0,1:T(8,128)}, f32[2816,64]{0,1:T(8,128)}, u32[]{:T(12...) while((bf16[1,2048,2816]{2,1,0:T(8,128)(2,1)}, ...), condition=%wide.windowed_dot_general_cond_rs.clone, body=%wide.windowed_dot_general_body_rs.clone.sunk | while | flops 2955968512 | bytes 108790456 | solution.py:20
  960.6 8.8 collective-permute-start.2
  981.6 8.7 collective-permute-start
  1022.6 8.7 collective-permute-start
  1063.5 7.8 collective-permute-start
  1101.3 161.4 %while.13 = (bf16[1,2048,2816]{2,1,0:T(8,128)(2,1)}, bf16[1,2048,1024]{1,2,0:T(8,128)(2,1)}, f32[2816,64]{0,1:T(8,128)}, f32[2816,64]{0,1:T(8,128)}, u32[]{:T(12...) while((bf16[1,2048,2816]{2,1,0:T(8,128)(2,1)}, ...), condition=%wide.windowed_dot_general_cond_rs.1.clone, body=%wide.windowed_dot_general_body_rs.1.clone.sunk | while | flops 2955968512 | bytes 108790456 | solution.py:20
  1102.2 8.7 collective-permute-start.4
  1122.1 8.8 collective-permute-start.6
  1143.1 8.7 collective-permute-start.4
  1184.0 7.8 collective-permute-start.4
  1224.0 8.7 collective-permute-start.4
  1262.8 8.7 collective-permute-start.27
  1294.7 38.7 %all-reduce.10 = f32[]{:T(128)} all-reduce(f32[]{:T(128)S(6)} %add.180), channel_id=13, replica_groups=mesh['rep'=1,'dp'=16] {'dp'}, use_global_device_ids=true, to_apply=%region_3.4.clone | all-reduce | flops 1 | bytes 8 | tf_op jit(solution)/vmap()/reduce_sum | solution.py:54
  1347.8 51.0 %all-gather.14.cloned.1.call-done = bf16[1,2,2816,1024]{3,2,1,0:T(8,128)(2,1)} async-done(((bf16[1,2,176,1024]{3,2,1,0:T(8,128)(2,1)}), bf16[1,2,2816,1024]{3,2,1,0:T(8,128)(2,1)}) %all-gather.14.cloned.1.call-update) | async-done | bytes 11534352 | tf_op jit(solution)/reshape | solution.py:58
  1398.8 61.9 %all-gather.12.cloned.1.call-done = bf16[1,2,1024,2816]{3,2,1,0:T(8,128)(2,1)} async-done(((bf16[1,2,64,2816]{3,2,1,0:T(8,128)(2,1)}), bf16[1,2,1024,2816]{3,2,1,0:T(8,128)(2,1)}) %all-gather.12.cloned.1.call-update) | async-done | bytes 11534352 | tf_op jit(solution)/reshape | solution.py:58
  1460.7 61.9 %all-gather.10.cloned.1.call-done = bf16[1,2,1024,2816]{3,2,1,0:T(8,128)(2,1)} async-done(((bf16[1,2,64,2816]{3,2,1,0:T(8,128)(2,1)}), bf16[1,2,1024,2816]{3,2,1,0:T(8,128)(2,1)}) %all-gather.10.cloned.1.call-update) | async-done | bytes 11534352 | tf_op jit(solution)/reshape | solution.py:58
  1522.6 11.7 copy.63
  (550 shorter events, 808.6 us)
Async XLA Ops:
  7.2 1391.6 %all-gather.14.cloned.1.call-start = ((), (), s32[]{:S(2)}) async-start(), calls=%async_computation.2 | async-start | bytes 12255232 | tf_op jit(solution)/reshape | solution.py:58
  149.7 13.7 collective-permute-start.16
  164.4 18.8 %collective-permute-start.18 = (f32[176,1024]{1,0:T(8,128)S(1)}, f32[176,1024]{1,0:T(8,128)S(1)}, u32[]{:S(2)}, u32[]{:S(2)}) collective-permute-start(f32[176,1024]{1,0:T(8,128)S(1)} %get-tuple-element.492), channel_id=31, source_target_pairs={{0,1},{1,2},{2,3},{3,4},{4,5},{5,6},{6,7},{7,8},{8,9},{9,10},{10,1... | collective-permute-start | bytes 2162696 | tf_op jit(solution)/vmap(transpose(jvp()))/dot_general | solution.py:9
  190.0 12.7 collective-permute-start.16
  207.1 12.9 collective-permute-start.18
  226.7 14.9 collective-permute-start.16
  246.3 12.7 collective-permute-start.18
  265.2 14.9 collective-permute-start.16
  284.9 12.7 collective-permute-start.18
  301.7 972.3 %collective-permute-start.28 = (f32[176,1024]{1,0:T(8,128)}, f32[176,1024]{1,0:T(8,128)}, u32[]{:S(2)}, u32[]{:S(2)}) collective-permute-start(f32[176,1024]{1,0:T(8,128)} %get-tuple-element.45), channel_id=32, source_target_pairs={{0,1},{1,2},{2,3},{3,4},{4,5},{5,6},{6,7},{7,8},{8,9},{9,10},{10,1... | collective-permute-start | bytes 2162696 | tf_op jit(solution)/vmap(transpose(jvp()))/dot_general | solution.py:9
  431.2 18.9 %collective-permute-start.22 = (f32[1024,176]{0,1:T(8,128)S(1)}, f32[1024,176]{0,1:T(8,128)S(1)}, u32[]{:S(2)}, u32[]{:S(2)}) collective-permute-start(f32[1024,176]{0,1:T(8,128)S(1)} %get-tuple-element.501), channel_id=37, source_target_pairs={{0,1},{1,2},{2,3},{3,4},{4,5},{5,6},{6,7},{7,8},{8,9},{9,10},{10,1... | collective-permute-start | bytes 2162696 | tf_op jit(solution)/vmap(transpose(jvp()))/dot_general | solution.py:9
  456.8 12.7 collective-permute-start.20
  473.7 12.7 collective-permute-start.22
  491.9 14.9 collective-permute-start.20
  529.6 14.9 collective-permute-start.20
  549.2 12.7 collective-permute-start.22
  567.0 708.6 %collective-permute-start.29 = (f32[1024,176]{0,1:T(8,128)}, f32[1024,176]{0,1:T(8,128)}, u32[]{:S(2)}, u32[]{:S(2)}) collective-permute-start(f32[1024,176]{0,1:T(8,128)} %get-tuple-element.47), channel_id=38, source_target_pairs={{0,1},{1,2},{2,3},{3,4},{4,5},{5,6},{6,7},{7,8},{8,9},{9,10},{10,1... | collective-permute-start | bytes 2162696 | tf_op jit(solution)/vmap(transpose(jvp()))/dot_general | solution.py:9
  592.3 16.4 %collective-permute-start.10 = (f32[2816,64]{0,1:T(8,128)S(1)}, f32[2816,64]{0,1:T(8,128)S(1)}, u32[]{:S(2)}, u32[]{:S(2)}) collective-permute-start(f32[2816,64]{0,1:T(8,128)S(1)} %get-tuple-element.474), channel_id=18, source_target_pairs={{0,1},{1,2},{2,3},{3,4},{4,5},{5,6},{6,7},{7,8},{8,9},{9,10},{10,1... | collective-permute-start | bytes 2162696 | tf_op jit(solution)/vmap(transpose(jvp()))/dot_general | solution.py:21
  619.1 15.4 collective-permute-start.8
  638.5 12.7 collective-permute-start.10
  658.4 17.2 %collective-permute-start.8 = (f32[2816,64]{0,1:T(8,128)}, f32[2816,64]{0,1:T(8,128)}, u32[]{:S(2)}, u32[]{:S(2)}) collective-permute-start(f32[2816,64]{0,1:T(8,128)} %broadcast_select_fusion.28), channel_id=16, source_target_pairs={{0,1},{1,2},{2,3},{3,4},{4,5},{5,6},{6,7},{7,8},{8,9},{9,10},{10,1... | collective-permute-start | bytes 2162696 | tf_op jit(solution)/vmap(transpose(jvp()))/dot_general | solution.py:21
  679.6 12.7 collective-permute-start.10
  699.5 15.9 %collective-permute-start.8 = (f32[2816,64]{0,1:T(8,128)}, f32[2816,64]{0,1:T(8,128)}, u32[]{:S(2)}, u32[]{:S(2)}) collective-permute-start(f32[2816,64]{0,1:T(8,128)} %broadcast_select_fusion.28), channel_id=16, source_target_pairs={{0,1},{1,2},{2,3},{3,4},{4,5},{5,6},{6,7},{7,8},{8,9},{9,10},{10,1... | collective-permute-start | bytes 2162696 | tf_op jit(solution)/vmap(transpose(jvp()))/dot_general | solution.py:21
  719.4 12.7 collective-permute-start.10
  737.1 541.0 %collective-permute-start.26 = (f32[2816,64]{0,1:T(8,128)}, f32[2816,64]{0,1:T(8,128)}, u32[]{:S(2)}, u32[]{:S(2)}) collective-permute-start(f32[2816,64]{0,1:T(8,128)} %get-tuple-element.41), channel_id=19, source_target_pairs={{0,1},{1,2},{2,3},{3,4},{4,5},{5,6},{6,7},{7,8},{8,9},{9,10},{10,1... | collective-permute-start | bytes 2162696 | tf_op jit(solution)/vmap(transpose(jvp()))/dot_general | solution.py:21
  796.4 16.4 %collective-permute-start.14 = (f32[2816,64]{0,1:T(8,128)S(1)}, f32[2816,64]{0,1:T(8,128)S(1)}, u32[]{:S(2)}, u32[]{:S(2)}) collective-permute-start(f32[2816,64]{0,1:T(8,128)S(1)} %get-tuple-element.483), channel_id=24, source_target_pairs={{0,1},{1,2},{2,3},{3,4},{4,5},{5,6},{6,7},{7,8},{8,9},{9,10},{10,1... | collective-permute-start | bytes 2162696 | tf_op jit(solution)/vmap(transpose(jvp()))/dot_general | solution.py:21
  823.1 15.3 collective-permute-start.12
  861.9 15.9 %collective-permute-start.12 = (f32[2816,64]{0,1:T(8,128)}, f32[2816,64]{0,1:T(8,128)}, u32[]{:S(2)}, u32[]{:S(2)}) collective-permute-start(f32[2816,64]{0,1:T(8,128)} %broadcast_select_fusion.30), channel_id=22, source_target_pairs={{0,1},{1,2},{2,3},{3,4},{4,5},{5,6},{6,7},{7,8},{8,9},{9,10},{10,1... | collective-permute-start | bytes 2162696 | tf_op jit(solution)/vmap(transpose(jvp()))/dot_general | solution.py:21
  881.8 12.7 collective-permute-start.14
  901.7 17.2 %collective-permute-start.12 = (f32[2816,64]{0,1:T(8,128)}, f32[2816,64]{0,1:T(8,128)}, u32[]{:S(2)}, u32[]{:S(2)}) collective-permute-start(f32[2816,64]{0,1:T(8,128)} %broadcast_select_fusion.30), channel_id=22, source_target_pairs={{0,1},{1,2},{2,3},{3,4},{4,5},{5,6},{6,7},{7,8},{8,9},{9,10},{10,1... | collective-permute-start | bytes 2162696 | tf_op jit(solution)/vmap(transpose(jvp()))/dot_general | solution.py:21
  922.9 12.7 collective-permute-start.14
  941.8 14.8 collective-permute-start
  960.6 12.7 collective-permute-start.2
  981.6 17.1 %collective-permute-start = (f32[2816,64]{0,1:T(8,128)}, f32[2816,64]{0,1:T(8,128)}, u32[]{:S(2)}, u32[]{:S(2)}) collective-permute-start(f32[2816,64]{0,1:T(8,128)} %broadcast_select_fusion.24), channel_id=3, source_target_pairs={{0,1},{1,2},{2,3},{3,4},{4,5},{5,6},{6,7},{7,8},{8,9},{9,10},{10,1... | collective-permute-start | bytes 2162696 | tf_op jit(solution)/vmap(transpose(jvp()))/dot_general | solution.py:20
  1002.7 12.7 collective-permute-start.2
  1022.6 17.0 %collective-permute-start = (f32[2816,64]{0,1:T(8,128)}, f32[2816,64]{0,1:T(8,128)}, u32[]{:S(2)}, u32[]{:S(2)}) collective-permute-start(f32[2816,64]{0,1:T(8,128)} %broadcast_select_fusion.24), channel_id=3, source_target_pairs={{0,1},{1,2},{2,3},{3,4},{4,5},{5,6},{6,7},{7,8},{8,9},{9,10},{10,1... | collective-permute-start | bytes 2162696 | tf_op jit(solution)/vmap(transpose(jvp()))/dot_general | solution.py:20
  1063.5 16.1 %collective-permute-start = (f32[2816,64]{0,1:T(8,128)}, f32[2816,64]{0,1:T(8,128)}, u32[]{:S(2)}, u32[]{:S(2)}) collective-permute-start(f32[2816,64]{0,1:T(8,128)} %broadcast_select_fusion.24), channel_id=3, source_target_pairs={{0,1},{1,2},{2,3},{3,4},{4,5},{5,6},{6,7},{7,8},{8,9},{9,10},{10,1... | collective-permute-start | bytes 2162696 | tf_op jit(solution)/vmap(transpose(jvp()))/dot_general | solution.py:20
  1083.6 12.7 collective-permute-start.2
  1102.2 15.9 %collective-permute-start.4 = (f32[2816,64]{0,1:T(8,128)}, f32[2816,64]{0,1:T(8,128)}, u32[]{:S(2)}, u32[]{:S(2)}) collective-permute-start(f32[2816,64]{0,1:T(8,128)} %broadcast_select_fusion.26), channel_id=9, source_target_pairs={{0,1},{1,2},{2,3},{3,4},{4,5},{5,6},{6,7},{7,8},{8,9},{9,10},{10,1... | collective-permute-start | bytes 2162696 | tf_op jit(solution)/vmap(transpose(jvp()))/dot_general | solution.py:20
  1122.1 12.7 collective-permute-start.6
  1143.1 17.0 %collective-permute-start.4 = (f32[2816,64]{0,1:T(8,128)}, f32[2816,64]{0,1:T(8,128)}, u32[]{:S(2)}, u32[]{:S(2)}) collective-permute-start(f32[2816,64]{0,1:T(8,128)} %broadcast_select_fusion.26), channel_id=9, source_target_pairs={{0,1},{1,2},{2,3},{3,4},{4,5},{5,6},{6,7},{7,8},{8,9},{9,10},{10,1... | collective-permute-start | bytes 2162696 | tf_op jit(solution)/vmap(transpose(jvp()))/dot_general | solution.py:20
  1164.2 12.7 collective-permute-start.6
  1184.0 16.1 %collective-permute-start.4 = (f32[2816,64]{0,1:T(8,128)}, f32[2816,64]{0,1:T(8,128)}, u32[]{:S(2)}, u32[]{:S(2)}) collective-permute-start(f32[2816,64]{0,1:T(8,128)} %broadcast_select_fusion.26), channel_id=9, source_target_pairs={{0,1},{1,2},{2,3},{3,4},{4,5},{5,6},{6,7},{7,8},{8,9},{9,10},{10,1... | collective-permute-start | bytes 2162696 | tf_op jit(solution)/vmap(transpose(jvp()))/dot_general | solution.py:20
  1224.0 17.0 %collective-permute-start.4 = (f32[2816,64]{0,1:T(8,128)}, f32[2816,64]{0,1:T(8,128)}, u32[]{:S(2)}, u32[]{:S(2)}) collective-permute-start(f32[2816,64]{0,1:T(8,128)} %broadcast_select_fusion.26), channel_id=9, source_target_pairs={{0,1},{1,2},{2,3},{3,4},{4,5},{5,6},{6,7},{7,8},{8,9},{9,10},{10,1... | collective-permute-start | bytes 2162696 | tf_op jit(solution)/vmap(transpose(jvp()))/dot_general | solution.py:20
  1262.8 16.4 %collective-permute-start.27 = (f32[2816,64]{0,1:T(8,128)}, f32[2816,64]{0,1:T(8,128)S(1)}, u32[]{:S(2)}, u32[]{:S(2)}) collective-permute-start(f32[2816,64]{0,1:T(8,128)} %get-tuple-element.43), channel_id=25, source_target_pairs={{0,1},{1,2},{2,3},{3,4},{4,5},{5,6},{6,7},{7,8},{8,9},{9,10},{10,1... | collective-permute-start | bytes 2162696 | tf_op jit(solution)/vmap(transpose(jvp()))/dot_general | solution.py:21
  1274.0 17.7 %collective-permute-start.25 = (f32[2816,64]{0,1:T(8,128)}, f32[2816,64]{0,1:T(8,128)S(1)}, u32[]{:S(2)}, u32[]{:S(2)}) collective-permute-start(f32[2816,64]{0,1:T(8,128)} %get-tuple-element.39), channel_id=12, source_target_pairs={{0,1},{1,2},{2,3},{3,4},{4,5},{5,6},{6,7},{7,8},{8,9},{9,10},{10,1... | collective-permute-start | bytes 2162696 | tf_op jit(solution)/vmap(transpose(jvp()))/dot_general | solution.py:20
  1338.8 121.9 %all-gather.12.cloned.1.call-start = ((), (), s32[]{:S(2)}) async-start(), calls=%async_computation.1 | async-start | bytes 12255232 | tf_op jit(solution)/reshape | solution.py:58
  1343.6 179.0 %all-gather.10.cloned.1.call-start = ((), (), s32[]{:S(2)}) async-start(), calls=%async_computation | async-start | bytes 12255232 | tf_op jit(solution)/reshape | solution.py:58
  (141 other events, 2092.4 us)
Sparse Core Ops, SparseCore 0:
  1338.9 59.8 all-gather.13
  1401.6 59.0 all-gather.11
  1463.5 59.0 all-gather.9
where the time goes:
time: 1560 us; the launch traced here: 1550 us
  starting transfers between devices  435 us (28%)
  matrix products  413 us (26%)
  waiting for transfers between devices  412 us (26%)
  other arithmetic  161 us (10%)
  local copies, waits for them, and re-layouts  75 us (5%)
  blocking collectives  38.7 us (2%)
  between operations  17 us (1%)
    reshape x3, waiting for transfers between devices, step(): t.reshape(-1, *t.shape[2:])  175 us
    dot_general x19, matrix products, matmul(): jnp.dot(a, w, preferred_element_type=jnp.float32).astype(jnp.bfloat16)  156 us
    dot_general x34, starting transfers between devices, matmul(): jnp.dot(a, w, preferred_element_type=jnp.float32).astype(jnp.bfloat16)  155 us
    dot_general x34, starting transfers between devices, layer(): up = jnp.dot(a, w['w_up'], preferred_element_type=jnp.float32)  147 us
    dot_general x19, matrix products, layer(): up = jnp.dot(a, w['w_up'], preferred_element_type=jnp.float32)  136 us
    dot_general x34, starting transfers between devices, layer(): gate = jnp.dot(a, w['w_gate'], preferred_element_type=jnp.float32)  133 us
    dot_general x19, matrix products, layer(): gate = jnp.dot(a, w['w_gate'], preferred_element_type=jnp.float32)  121 us
    dot_general x34, waiting for transfers between devices, layer(): gate = jnp.dot(a, w['w_gate'], preferred_element_type=jnp.float32)  88.4 us
  transfers between devices with their start and end apart: 105, of which 80 were waited for; matrix products, arithmetic and copies ran while one was open for 30% of the time, Pallas kernels for 0%

commit v1 on v0

v1 whole, which is shorter than its diff:
```python
import jax
import jax.numpy as jnp
from jax import lax
from jax.sharding import PartitionSpec as P

NAMES = ("w_gate", "w_up", "w_down")


def dot(a, b, dims):
    return lax.dot_general(a, b, (dims, ((), ())), preferred_element_type=jnp.float32)


def adamw(w, m, v, g):
    m = 0.9 * m + 0.1 * g
    v = 0.95 * v + 0.05 * g * g
    step = m * lax.rsqrt(v + 1e-8) + 0.1 * w
    return (w - 0.02 * step).astype(jnp.bfloat16), m, v


def solution(mesh):
    n = mesh.shape["dp"]

    def step(x, dy, w_gate, w_up, w_down, *moments):
        m, v = moments[:3], moments[3:]
        layers = w_gate.shape[0]
        h = x[0]
        saved = []
        for l in range(layers):
            wide = h.astype(jnp.float32)
            scale = lax.rsqrt(jnp.mean(wide**2, -1, keepdims=True) + 1e-6)
            a = (wide * scale).astype(jnp.bfloat16)
            gate = dot(a, w_gate[l], ((1,), (0,)))
            up = dot(a, w_up[l], ((1,), (0,)))
            z = (jax.nn.silu(gate) * up).astype(jnp.bfloat16)
            saved.append((h, scale, a, gate, up, z))
            if l + 1 < layers:
                h = h + dot(z, w_down[l], ((1,), (0,))).astype(jnp.bfloat16)
        d = dy[0]
        shards = {name: [None] * layers for name in NAMES}

        def scatter(t):
            return lax.psum_scatter(t.astype(jnp.bfloat16), "dp", scatter_dimension=0, tiled=True)

        for l in reversed(range(layers)):
            h, scale, a, gate, up, z = saved[l]
            shards["w_down"][l] = scatter(dot(z, d, ((0,), (0,))))
            dz = dot(d, w_down[l], ((1,), (1,))).astype(jnp.bfloat16).astype(jnp.float32)
            sig = jax.nn.sigmoid(gate)
            silu = gate * sig
            dup = (dz * silu).astype(jnp.bfloat16)
            dgate = (dz * up * (sig * (1 + gate * (1 - sig)))).astype(jnp.bfloat16)
            shards["w_gate"][l] = scatter(dot(a, dgate, ((0,), (0,))))
            shards["w_up"][l] = scatter(dot(a, dup, ((0,), (0,))))
            if l:
                da = dot(dgate, w_gate[l], ((1,), (1,))) + dot(dup, w_up[l], ((1,), (1,)))
                wide = h.astype(jnp.float32)
                back = da * scale - wide * (scale**3 * jnp.mean(da * wide, -1, keepdims=True))
                d = d + back.astype(jnp.bfloat16)

        g = [[t.astype(jnp.float32) for t in shards[name]] for name in NAMES]
        total = lax.psum(sum(jnp.sum(t * t) for ts in g for t in ts), "dp")
        count = sum(t.size for ts in g for t in ts) * n
        factor = jnp.minimum(1.0, 0.5 * lax.rsqrt(total / count + 1e-30))
        me = lax.axis_index("dp")
        new = []
        for w, mm, vv, ts in zip((w_gate, w_up, w_down), m, v, g, strict=True):
            rows = mm.shape[1]
            own = lax.dynamic_slice_in_dim(w, me * rows, rows, 1).astype(jnp.float32)
            nw, nm, nv = adamw(own, mm, vv, jnp.stack(ts) * factor)
            new.append((lax.all_gather(nw, "dp", axis=1, tiled=True), nm, nv))
        return tuple(one[which] for which in range(3) for one in new)

    seq, whole, rows = P(("rep", "dp"), None, None), P(), P(None, "dp", None)
    return jax.shard_map(
        step,
        mesh=mesh,
        in_specs=(seq, seq) + (whole,) * 3 + (rows,) * 6,
        out_specs=(P("rep", None, None),) * 3 + (P("rep", "dp", None),) * 6,
        check_vma=False,
    )
```

time: 1560 us -> 890 us (0.57)
  starting transfers between devices: 435 us -> 0.37 us
  other arithmetic: 161 us -> 36.2 us
  matrix products: 413 us -> 326 us
  local copies, waits for them, and re-layouts: 75 us -> 37.5 us
  waiting for transfers between devices: 412 us -> 431 us
    dot_general x102 -> x0, starting transfers between devices: 435 us -> none  [the longest x34 155 us: matmul(): jnp.dot(a, w, preferred_element_type=jnp.float32).astype(jnp.bfloat16)]
    reduce_scatter x0 -> x6, waiting for transfers between devices: none -> 258 us  [scatter(): lax.psum_scatter(t.astype(jnp.bfloat16), 'dp', scatter_dimension=0, tiled...]
    dot_general x102 -> x0, waiting for transfers between devices: 238 us -> none  [the longest x34 88.4 us: layer(): gate = jnp.dot(a, w['w_gate'], preferred_element_type=jnp.float32)]
    reshape x3 -> x0, waiting for transfers between devices: 175 us -> none  [step(): t.reshape(-1, *t.shape[2:])]
    all_gather x0 -> x3, waiting for transfers between devices: none -> 173 us  [step(): new.append((lax.all_gather(nw, 'dp', axis=1, tiled=True), nm, nv))]
    dot_general x112 -> x0, other arithmetic: 126 us -> none
    dot_general x57 -> x15, matrix products: 413 us -> 326 us  [dot(): lax.dot_general(a, b, (dims, ((), ())), preferred_element_type=jnp.float32)]
    reduce_sum x1 -> x0, blocking collectives: 38.7 us -> none  [of_a_group(): jnp.sum(g * g)]
  transfers between devices with their start and end apart: 105 -> 9, of which waited for: 80 -> 7; matrix products, arithmetic and copies ran while one was open for 30% -> 23% of each run, Pallas kernels for 0% -> 0%
where the time goes in v1:
time: 890 us; the launch traced here: 884 us
  waiting for transfers between devices  431 us (48%)
  matrix products  326 us (37%)
  local copies, waits for them, and re-layouts  37.5 us (4%)
  other arithmetic  36.2 us (4%)
  blocking collectives  33.3 us (4%)
  between operations  19.1 us (2%)
    dot_general x15, matrix products, dot(): lax.dot_general(a, b, (dims, ((), ())), preferred_element_type=jnp.float32)  326 us
    reduce_scatter x6, waiting for transfers between devices, scatter(): lax.psum_scatter(t.astype(jnp.bfloat16), 'dp', scatter_dimension=0, tiled...  258 us
    all_gather x3, waiting for transfers between devices, step(): new.append((lax.all_gather(nw, 'dp', axis=1, tiled=True), nm, nv))  173 us
    unnamed x43, local copies, waits for them, and re-layouts  37.5 us
    psum x1, blocking collectives, step(): total = lax.psum(sum((jnp.sum(t * t) for ts in g for t in ts)), 'dp')  33.3 us
  transfers between devices with their start and end apart: 9, of which 7 were waited for; matrix products, arithmetic and copies ran while one was open for 23% of the time, Pallas kernels for 0%

profile of v1, /device:TPU:0, one launch (start us, length us, event | category | flops | bytes accessed | tf_op | source)
XLA Modules:
  0.0 883.8 jit_solution(10410823689446441827)
XLA Ops:
  7.2 6.5 copy.20
  13.7 3.1 fusion.13
  16.8 19.8 %fusion.33 = f32[2048,2816]{1,0:T(8,128)} fusion(bf16[2,1024,2816]{2,1,0:T(8,128)(2,1)} %param.13, bf16[1,2048,1024]{2,1,0:T(8,128)(2,1)} %param.11, f32[2048]{0:T(1024)S(1)} %add_rsqrt_fusion.1), kind=kOutput, calls=%fused_computation.48 | convolution fusion | flops 11817451520 | bytes 33038336 | tf_op jit(solution)/shard_map/dot_general | solution.py:10
  36.7 28.7 %multiply_convert_fusion.1 = (bf16[2048,2816]{1,0:T(8,128)(2,1)}, f32[2048,2816]{1,0:T(8,128)}) fusion(f32[2048,2816]{1,0:T(8,128)} %fusion.33, bf16[2,1024,2816]{2,1,0:T(8,128)(2,1)} %param.14, bf16[1,2048,1024]{2,1,0:T(8,128)(2,1)} %param.11, f32[2048]{0:T(1024)S(1)} %add_rsqrt_fusion.1), kind=kOutput, calls=%fused_computation.13 | convolution fusion | flops 11852054528 | bytes 67641344 | tf_op jit(solution)/shard_map/dot_general | solution.py:10
  65.3 20.0 %fusion.15 = (f32[2048]{0:T(1024)S(1)}, bf16[2048,1024]{0,1:T(8,128)(2,1)}) fusion(bf16[2048,2816]{1,0:T(8,128)(2,1)} %get-tuple-element.20, bf16[2,2816,1024]{2,1,0:T(8,128)(2,1)} %param.15, bf16[1,2048,1024]{1,2,0:T(8,128)(2,1)} %copy.20), kind=kOutput, calls=%fused_computation.29 | convolution fusion | flops 11821643776 | bytes 25698304 | tf_op jit(solution)/shard_map/dot_general | solution.py:10
  85.3 20.3 %fusion.22 = f32[2048,2816]{1,0:T(8,128)} fusion(bf16[2,1024,2816]{2,1,0:T(8,128)(2,1)} %param.13, bf16[2048,1024]{0,1:T(8,128)(2,1)} %get-tuple-element.23, f32[2048]{0:T(1024)S(1)} %add_rsqrt_fusion), kind=kOutput, calls=%fused_computation.37 | convolution fusion | flops 11817451520 | bytes 33038336 | tf_op jit(solution)/shard_map/dot_general | solution.py:10
  105.6 18.1 %fusion.26 = f32[2048,2816]{1,0:T(8,128)} fusion(bf16[2,1024,2816]{2,1,0:T(8,128)(2,1)} %param.14, bf16[2048,1024]{0,1:T(8,128)(2,1)S(1)} %copy-done.3, f32[2048]{0:T(1024)S(1)} %add_rsqrt_fusion), kind=kOutput, calls=%fused_computation.41 | convolution fusion | flops 11817451520 | bytes 33038336 | tf_op jit(solution)/shard_map/dot_general | solution.py:10
  123.7 33.9 %fusion.2 = (bf16[2048,2816]{1,0:T(8,128)(2,1)}, bf16[2048,2816]{1,0:T(8,128)(2,1)}) fusion(f32[2048,2816]{1,0:T(8,128)} %fusion.22, f32[2048,2816]{1,0:T(8,128)} %fusion.26, bf16[2,2816,1024]{2,1,0:T(8,128)(2,1)} %param.15, bf16[1,2048,1024]{2,1,0:T(8,128)(2,1)} %param.12), kind=kOutput, calls=%fused_computation.6 | convolution fusion | flops 11897667584 | bytes 79167488 | tf_op jit(solution)/shard_map/dot_general | solution.py:10
  157.6 18.5 %convolution_convert_fusion.4 = bf16[1024,2816]{1,0:T(8,128)(2,1)} fusion(bf16[2048,2816]{1,0:T(8,128)(2,1)} %get-tuple-element.19, bf16[2048,1024]{0,1:T(8,128)(2,1)} %get-tuple-element.23, f32[2048]{0:T(1024)S(1)} %add_rsqrt_fusion), kind=kOutput, calls=%fused_computation.59 | convolution fusion | flops 11820335104 | bytes 21504000 | tf_op jit(solution)/shard_map/dot_general | solution.py:10
  176.2 6.9 copy.21
  183.1 18.7 %fusion.20 = f32[2048,1024]{0,1:T(8,128)} fusion(bf16[2048,2816]{1,0:T(8,128)(2,1)} %get-tuple-element.19, bf16[2,1024,2816]{2,1,0:T(8,128)(2,1)} %param.13), kind=kOutput, calls=%fused_computation.35 | convolution fusion | flops 11811160064 | bytes 25690112 | tf_op jit(solution)/shard_map/dot_general | solution.py:10
  201.8 21.2 %fusion.17 = (f32[2048]{0:T(1024)S(1)}, f32[2048,1024]{0,1:T(8,128)}) fusion(bf16[2048,1024]{0,1:T(8,128)(2,1)} %get-tuple-element.23, f32[2048,1024]{0,1:T(8,128)} %fusion.20, bf16[2048,2816]{1,0:T(8,128)(2,1)} %get-tuple-element.18, bf16[2,1024,2816]{2,1,0:T(8,128)(2,1)} %param.14), kind=kOutput, calls=%fused_computation.31 | convolution fusion | flops 11819546624 | bytes 38281216 | tf_op jit(solution)/shard_map/dot_general | solution.py:10
  223.1 5.9 fusion.56
  229.1 18.8 %convolution_convert_fusion = bf16[2048,2816]{1,0:T(8,128)(2,1)} fusion(bf16[2048,1024]{0,1:T(8,128)(2,1)S(1)} %fusion.56, bf16[2,2816,1024]{2,1,0:T(8,128)(2,1)} %param.15), kind=kOutput, calls=%fused_computation.23 | convolution fusion | flops 11816927232 | bytes 21495808 | tf_op jit(solution)/shard_map/dot_general | solution.py:10
  247.9 25.0 %fusion.40 = bf16[1024,2816]{1,0:T(8,128)(2,1)} fusion(f32[2048,2816]{1,0:T(8,128)} %get-tuple-element.21, bf16[2048,2816]{1,0:T(8,128)(2,1)} %convolution_convert_fusion, f32[2048,2816]{1,0:T(8,128)} %fusion.33, bf16[1,2048,1024]{1,2,0:T(8,128)(2,1)S(1)} %copy-done, f32[2048]{0:T(1024)S(1)} %copy-done.15), kind=kOutput, calls=%fused_computation.55 | convolution fusion | flops 11883773952 | bytes 67641344 | tf_op jit(solution)/shard_map/dot_general | solution.py:10
  272.8 0.0 reduce-scatter.11.cloned.1.call-start
  272.9 22.8 %fusion.43 = bf16[1024,2816]{1,0:T(8,128)(2,1)} fusion(bf16[2048,2816]{1,0:T(8,128)(2,1)} %convolution_convert_fusion, f32[2048,2816]{1,0:T(8,128)} %fusion.33, bf16[1,2048,1024]{1,2,0:T(8,128)(2,1)} %copy.20, f32[2048]{0:T(1024)S(1)} %copy-done.15), kind=kOutput, calls=%fused_computation.56 | convolution fusion | flops 11860705280 | bytes 44572672 | tf_op jit(solution)/shard_map/dot_general | solution.py:10
  295.7 0.0 reduce-scatter.13.cloned.1.call-start
  295.7 18.8 %convolution_convert_fusion.3 = bf16[1024,2816]{1,0:T(8,128)(2,1)} fusion(bf16[2048,2816]{1,0:T(8,128)(2,1)} %get-tuple-element.18, bf16[2048,1024]{0,1:T(8,128)(2,1)} %get-tuple-element.23, f32[2048]{0:T(1024)S(1)} %copy-done.11), kind=kOutput, calls=%fused_computation.58 | convolution fusion | flops 11820335104 | bytes 21504000 | tf_op jit(solution)/shard_map/dot_general | solution.py:10
  314.6 17.9 %convolution_convert_fusion.2 = bf16[2816,1024]{1,0:T(8,128)(2,1)} fusion(bf16[2048,2816]{1,0:T(8,128)(2,1)} %get-tuple-element.20, bf16[2048,1024]{0,1:T(8,128)(2,1)} %copy-done.4), kind=kOutput, calls=%fused_computation.57 | convolution fusion | flops 11814043648 | bytes 21495808 | tf_op jit(solution)/shard_map/dot_general | solution.py:10
  332.5 23.7 %fusion.39 = bf16[2816,1024]{1,0:T(8,128)(2,1)} fusion(f32[2048,2816]{1,0:T(8,128)} %fusion.26, bf16[1,2048,1024]{2,1,0:T(8,128)(2,1)} %param.12, f32[2048,2816]{1,0:T(8,128)} %fusion.22), kind=kOutput, calls=%fused_computation.54 | convolution fusion | flops 11848646656 | bytes 56098816 | tf_op jit(solution)/shard_map/dot_general | solution.py:10
  356.4 1.9 fusion.84
  358.3 1.8 fusion.83
  361.4 53.7 %reduce-scatter.11.cloned.1.call-done = bf16[64,2816]{1,0:T(8,128)(2,1)} async-done(((bf16[1024,2816]{1,0:T(8,128)(2,1)}), bf16[64,2816]{1,0:T(8,128)(2,1)}) %reduce-scatter.11.cloned.1.call-update) | async-done | bytes 360464 | tf_op jit(solution)/shard_map/reduce_scatter | solution.py:42
  415.2 1.8 fusion.85
  417.6 68.0 %reduce-scatter.13.cloned.1.call-done = bf16[64,2816]{1,0:T(8,128)(2,1)} async-done(((bf16[1024,2816]{1,0:T(8,128)(2,1)}), bf16[64,2816]{1,0:T(8,128)(2,1)}) %reduce-scatter.13.cloned.1.call-update) | async-done | bytes 360464 | tf_op jit(solution)/shard_map/reduce_scatter | solution.py:42
  485.6 1.8 fusion.86
  488.0 69.0 %reduce-scatter.15.cloned.1.call-done = bf16[176,1024]{1,0:T(8,128)(2,1)} async-done(((bf16[2816,1024]{1,0:T(8,128)(2,1)}), bf16[176,1024]{1,0:T(8,128)(2,1)}) %reduce-scatter.15.cloned.1.call-update) | async-done | bytes 360464 | tf_op jit(solution)/shard_map/reduce_scatter | solution.py:42
  557.0 1.8 fusion.87
  559.4 67.5 %reduce-scatter.17.cloned.1.call-done = bf16[176,1024]{1,0:T(8,128)(2,1)} async-done(((bf16[2816,1024]{1,0:T(8,128)(2,1)}), bf16[176,1024]{1,0:T(8,128)(2,1)}) %reduce-scatter.17.cloned.1.call-update) | async-done | bytes 360464 | tf_op jit(solution)/shard_map/reduce_scatter | solution.py:42
  626.9 1.8 fusion.88
  629.4 33.3 %psum.7 = f32[]{:T(128)} all-reduce(f32[]{:T(128)S(6)} %add.135), channel_id=1, replica_groups=mesh['rep'=1,'dp'=16] {'dp'}, use_global_device_ids=true, to_apply=%region_15.16 | all-reduce | flops 1 | bytes 8 | tf_op jit(solution)/shard_map/psum | solution.py:61
  663.4 1.0 convert_bitcast_fusion
  664.4 1.1 convert_bitcast_fusion.1
  665.5 3.5 fusion.79
  669.1 1.2 convert_bitcast_fusion.2
  670.2 1.0 convert_bitcast_fusion.3
  671.3 4.2 fusion.76
  675.6 1.0 convert_bitcast_fusion.5
  676.7 3.3 fusion.73
  680.0 49.0 %all-gather.8.cloned.1.call-done = bf16[2,2816,1024]{2,1,0:T(8,128)(2,1)} async-done(((bf16[2,176,1024]{2,1,0:T(8,128)(2,1)}), bf16[2,2816,1024]{2,1,0:T(8,128)(2,1)}) %all-gather.8.cloned.1.call-update) | async-done | bytes 11534352 | tf_op jit(solution)/shard_map/all_gather | solution.py:70
  729.0 61.9 %all-gather.6.cloned.1.call-done = bf16[2,1024,2816]{2,1,0:T(8,128)(2,1)} async-done(((bf16[2,64,2816]{2,1,0:T(8,128)(2,1)}), bf16[2,1024,2816]{2,1,0:T(8,128)(2,1)}) %all-gather.6.cloned.1.call-update) | async-done | bytes 11534352 | tf_op jit(solution)/shard_map/all_gather | solution.py:70
  790.9 61.9 %all-gather.4.cloned.1.call-done = bf16[2,1024,2816]{2,1,0:T(8,128)(2,1)} async-done(((bf16[2,64,2816]{2,1,0:T(8,128)(2,1)}), bf16[2,1024,2816]{2,1,0:T(8,128)(2,1)}) %all-gather.4.cloned.1.call-update) | async-done | bytes 11534352 | tf_op jit(solution)/shard_map/all_gather | solution.py:70
  852.8 11.7 %copy.25 = bf16[2,1024,2816]{2,1,0:T(8,128)(2,1)} copy(bf16[2,1024,2816]{2,1,0:T(8,128)(2,1)} %all-gather.4.cloned.1.call-done) | data formatting | bytes 23068672
  864.5 5.8 copy.26
  870.4 0.8 slice-done.1
  871.1 1.2 slice-done.2
  872.4 4.4 copy.27
  (59 shorter events, 0.6 us)
Async XLA Ops:
  7.2 349.2 %reduce-scatter.9.cloned.1.call-start = ((), (), s32[]{:S(2)}) async-start(), calls=%async_computation.7 | async-start | bytes 6127616 | tf_op jit(solution)/shard_map/reduce_scatter | solution.py:42
  16.8 19.8 %copy-start.14 = (f32[2048]{0:T(1024)}, f32[2048]{0:T(1024)S(1)}, u32[]{:S(2)}) copy-start(f32[2048]{0:T(1024)S(1)} %add_rsqrt_fusion.1) | copy-start | bytes 24580
  85.3 20.3 %copy-start.12 = (f32[2048]{0:T(1024)}, f32[2048]{0:T(1024)S(1)}, u32[]{:S(2)}) copy-start(f32[2048]{0:T(1024)S(1)} %get-tuple-element.22) | copy-start | bytes 24580
  85.3 137.8 %copy-start.10 = (f32[2048]{0:T(1024)}, f32[2048]{0:T(1024)S(1)}, u32[]{:S(2)}) copy-start(f32[2048]{0:T(1024)S(1)} %add_rsqrt_fusion) | copy-start | bytes 24580
  85.3 20.3 %copy-start.3 = (bf16[2048,1024]{0,1:T(8,128)(2,1)S(1)}, bf16[2048,1024]{0,1:T(8,128)(2,1)}, u32[]{:S(2)}) copy-start(bf16[2048,1024]{0,1:T(8,128)(2,1)} %get-tuple-element.23) | copy-start | bytes 12582916
  176.2 182.2 %reduce-scatter.7.cloned.1.call-start = ((), (), s32[]{:S(2)}) async-start(), calls=%async_computation.6 | async-start | bytes 6127616 | tf_op jit(solution)/shard_map/reduce_scatter | solution.py:42
  201.8 21.2 %copy-start.13 = (f32[2048]{0:T(1024)S(1)}, f32[2048]{0:T(1024)}, u32[]{:S(2)}) copy-start(f32[2048]{0:T(1024)} %copy-done.12) | copy-start | bytes 24580
  201.8 21.2 %copy-start.1 = (bf16[1,2048,1024]{1,2,0:T(8,128)(2,1)S(1)}, bf16[1,2048,1024]{1,2,0:T(8,128)(2,1)}, u32[]{:S(2)}) copy-start(bf16[1,2048,1024]{1,2,0:T(8,128)(2,1)} %copy.21) | copy-start | bytes 12582916
  229.0 18.8 %copy-start.4 = (bf16[2048,1024]{0,1:T(8,128)(2,1)}, bf16[2048,1024]{0,1:T(8,128)(2,1)S(1)}, u32[]{:S(2)}) copy-start(bf16[2048,1024]{0,1:T(8,128)(2,1)S(1)} %fusion.56) | copy-start | bytes 12582916
  229.0 18.8 %copy-start = (bf16[1,2048,1024]{1,2,0:T(8,128)(2,1)S(1)}, bf16[1,2048,1024]{1,2,0:T(8,128)(2,1)}, u32[]{:S(2)}) copy-start(bf16[1,2048,1024]{1,2,0:T(8,128)(2,1)} %copy.20) | copy-start | bytes 12582916
  229.1 18.8 %copy-start.15 = (f32[2048]{0:T(1024)S(1)}, f32[2048]{0:T(1024)}, u32[]{:S(2)}) copy-start(f32[2048]{0:T(1024)} %copy-done.14) | copy-start | bytes 24580
  272.8 22.9 %copy-start.11 = (f32[2048]{0:T(1024)S(1)}, f32[2048]{0:T(1024)}, u32[]{:S(2)}) copy-start(f32[2048]{0:T(1024)} %copy-done.10) | copy-start | bytes 24580
  272.8 142.3 %reduce-scatter.11.cloned.1.call-start = ((), (), s32[]{:S(2)}) async-start(), calls=%async_computation.8 | async-start | bytes 6127616 | tf_op jit(solution)/shard_map/reduce_scatter | solution.py:42
  295.7 189.9 %reduce-scatter.13.cloned.1.call-start = ((), (), s32[]{:S(2)}) async-start(), calls=%async_computation.9 | async-start | bytes 6127616 | tf_op jit(solution)/shard_map/reduce_scatter | solution.py:42
  314.5 242.5 %reduce-scatter.15.cloned.1.call-start = ((), (), s32[]{:S(2)}) async-start(), calls=%async_computation.10 | async-start | bytes 6127616 | tf_op jit(solution)/shard_map/reduce_scatter | solution.py:42
  332.5 294.5 %reduce-scatter.17.cloned.1.call-start = ((), (), s32[]{:S(2)}) async-start(), calls=%async_computation.11 | async-start | bytes 6127616 | tf_op jit(solution)/shard_map/reduce_scatter | solution.py:42
  356.3 309.2 %copy-start.5 = (f32[2,176,1024]{2,1,0:T(8,128)S(1)}, f32[2,176,1024]{2,1,0:T(8,128)}, u32[]{:S(2)}) copy-start(f32[2,176,1024]{2,1,0:T(8,128)} %param.21) | copy-start | bytes 4325380
  356.3 309.2 %copy-start.6 = (f32[2,176,1024]{2,1,0:T(8,128)S(1)}, f32[2,176,1024]{2,1,0:T(8,128)}, u32[]{:S(2)}) copy-start(f32[2,176,1024]{2,1,0:T(8,128)} %param.18) | copy-start | bytes 4325380
  356.3 372.7 %all-gather.8.cloned.1.call-start = ((), (), s32[]{:S(2)}) async-start(), calls=%async_computation.14 | async-start | bytes 12255232 | tf_op jit(solution)/shard_map/all_gather | solution.py:70
  665.5 10.1 %copy-start.9 = (bf16[64,2816]{1,0:T(8,128)(2,1)S(1)}, bf16[64,2816]{1,0:T(8,128)(2,1)}, u32[]{:S(2)}) copy-start(bf16[64,2816]{1,0:T(8,128)(2,1)} %reduce-scatter.9.cloned.1.call-done) | copy-start | bytes 1081348
  669.0 7.7 copy-start.7
  669.0 7.7 copy-start.8
  669.0 121.9 %all-gather.6.cloned.1.call-start = ((), (), s32[]{:S(2)}) async-start(), calls=%async_computation.13 | async-start | bytes 12255232 | tf_op jit(solution)/shard_map/all_gather | solution.py:70
  675.5 177.3 %all-gather.4.cloned.1.call-start = ((), (), s32[]{:S(2)}) async-start(), calls=%async_computation.12 | async-start | bytes 12255232 | tf_op jit(solution)/shard_map/all_gather | solution.py:70
  852.8 11.7 %copy-start.2 = (bf16[2,1024,2816]{2,1,0:T(8,128)(2,1)S(1)}, bf16[2,1024,2816]{2,1,0:T(8,128)(2,1)}, u32[]{:S(2)}) copy-start(bf16[2,1024,2816]{2,1,0:T(8,128)(2,1)} %all-gather.6.cloned.1.call-done) | copy-start | bytes 34603012
  852.8 17.5 %slice-start = ((s8[11534336]{0:T(1024)(128)(4,1)}), s8[4194304]{0:T(1024)(128)(4,1)S(1)}, s32[]{:S(2)}) async-start(s8[11534336]{0:T(1024)(128)(4,1)} %bitcast.78), calls=%async_computation.15 | async-start | bytes 8388608
  852.8 18.3 %slice-start.1 = ((s8[11534336]{0:T(1024)(128)(4,1)}), s8[4194304]{0:T(1024)(128)(4,1)S(1)}, s32[]{:S(2)}) async-start(s8[11534336]{0:T(1024)(128)(4,1)} %bitcast.78), calls=%async_computation.16 | async-start | bytes 8388608
  864.5 7.9 slice-start.2
Sparse Core Ops, SparseCore 0:
  176.3 69.6 reduce-scatter.8
  272.9 69.6 reduce-scatter.6
  345.0 70.1 reduce-scatter.10
  417.9 67.6 reduce-scatter.12
  488.3 68.6 reduce-scatter.14
  559.7 67.1 reduce-scatter.16
  669.1 59.8 all-gather.7
  731.9 59.0 all-gather.5
  793.8 59.0 all-gather.3

commit v2 on v1

--- a/solution.py
+++ b/solution.py
@@ -1,7 +1,13 @@
+import functools
+
 import jax
 import jax.numpy as jnp
 from jax import lax
+from jax.experimental import pallas as pl
+from jax.experimental.pallas import tpu as pltpu
 from jax.sharding import PartitionSpec as P
+
+MESH = pl.DeviceIdType.MESH
 
 NAMES = ("w_gate", "w_up", "w_down")
 
@@ -10,11 +16,157 @@
     return lax.dot_general(a, b, (dims, ((), ())), preferred_element_type=jnp.float32)
 
 
-def adamw(w, m, v, g):
-    m = 0.9 * m + 0.1 * g
-    v = 0.95 * v + 0.05 * g * g
-    step = m * lax.rsqrt(v + 1e-8) + 0.1 * w
-    return (w - 0.02 * step).astype(jnp.bfloat16), m, v
+LINKS = (8, 4, 2)
+
+
+def flipped(me, stride):
+    return me + stride - 2 * stride * ((me // stride) % 2)
+
+
+def widths(columns, turn):
+    lanes = columns // 128
+    sizes = [128 * ((lanes + (k + turn) % 3) // 3) for k in range(3)]
+    starts = [0, sizes[0], sizes[0] + sizes[1]]
+    return list(zip(starts, sizes))
+
+
+def gather_kernel(shapes, count, sq, *refs):
+    n_mat = len(shapes)
+    g, w, m, v, new_w, new_m, new_v, own_w, out_w, out_m, out_v = (refs[i * n_mat : (i + 1) * n_mat] for i in range(11))
+    squares, sq_send, sq_recv, in_sem, keep_sem, mv_sem, ici_send, ici_recv, d2d_send, d2d_recv = refs[11 * n_mat :]
+    me = lax.axis_index("dp")
+    at = [(me // s) % 2 for s in LINKS]
+    core = me % 2
+    units = [(i, l) for l in reversed(range(shapes[0][0])) for i in range(n_mat)]
+
+    loads = [pltpu.make_async_copy(w[i].at[l, me], own_w[i].at[l], in_sem.at[u]) for u, (i, l) in enumerate(units)]
+    for copy in loads:
+        copy.start()
+    barrier = pltpu.get_barrier_semaphore()
+    for k in range(1, 16):
+        pl.semaphore_signal(barrier, inc=1, device_id={"dp": (me + k) % 16}, device_id_type=MESH)
+    pl.semaphore_wait(barrier, 15)
+
+    sends = []
+    for k in range(1, 16):
+        copy = pltpu.make_async_remote_copy(
+            sq, squares.at[me], sq_send.at[k], sq_recv.at[k], device_id={"dp": (me + k) % 16}, device_id_type=MESH
+        )
+        copy.start()
+        sends.append(copy)
+    squares[me] = sq[...]
+    for copy in sends:
+        copy.wait_recv()
+    total = jnp.sum(jnp.sum(squares[...], axis=0), axis=(0, 1), keepdims=True)
+    factor = jnp.minimum(1.0, 0.5 * lax.rsqrt(total / count + 1e-30))
+
+    def ici(u, k, phase, i, l, cols):
+        p, q, r = k, (k + 1) % 3, (k + 2) % 3
+        where = list(at)
+        for d in (p, q)[:phase]:
+            where[d] = pl.ds(0, 2)
+        there = new_w[i].at[l, where[0], where[1], where[2], core, :, pl.ds(*cols)]
+        here = out_w[i].at[l, :, pl.ds(*cols)] if phase == 0 else there
+        return pltpu.make_async_remote_copy(
+            here,
+            there,
+            ici_send.at[3 * u + k, phase],
+            ici_recv.at[3 * u + k, phase],
+            device_id={"dp": flipped(me, LINKS[(p, q, r)[phase]])},
+            device_id_type=MESH,
+        )
+
+    def d2d(u, k, piece, i, l, cols):
+        order = (k, (k + 1) % 3, (k + 2) % 3)
+        where = list(at)
+        for d in order[: max(piece - 1, 0)]:
+            where[d] = pl.ds(0, 2)
+        if piece:
+            where[order[piece - 1]] = 1 - at[order[piece - 1]]
+        there = new_w[i].at[l, where[0], where[1], where[2], core, :, pl.ds(*cols)]
+        here = out_w[i].at[l, :, pl.ds(*cols)] if piece == 0 else there
+        return pltpu.make_async_remote_copy(
+            here,
+            there,
+            d2d_send.at[3 * u + k, piece],
+            d2d_recv.at[3 * u + k, piece],
+            device_id={"dp": flipped(me, 1)},
+            device_id_type=MESH,
+        )
+
+    moved, kept, stores = [], [], []
+    for u, (i, l) in enumerate(units):
+        loads[u].wait()
+        clipped = g[i][l].astype(jnp.float32) * factor
+        mm = 0.9 * m[i][l] + 0.1 * clipped
+        vv = 0.95 * v[i][l] + 0.05 * clipped * clipped
+        old = own_w[i][l].astype(jnp.float32)
+        out_w[i][l] = (old - 0.02 * (mm * lax.rsqrt(vv + 1e-8) + 0.1 * old)).astype(jnp.bfloat16)
+        out_m[i][l] = mm
+        out_v[i][l] = vv
+        for k, cols in enumerate(widths(shapes[i][2], u)):
+            for copy in (ici(u, k, 0, i, l, cols), d2d(u, k, 0, i, l, cols)):
+                copy.start()
+                moved.append(copy)
+        keep = pltpu.make_async_copy(out_w[i].at[l], new_w[i].at[l, at[0], at[1], at[2], core], keep_sem.at[u])
+        keep.start()
+        kept.append(keep)
+        for j, (out, new) in enumerate(((out_m, new_m), (out_v, new_v))):
+            store = pltpu.make_async_copy(out[i].at[l], new[i].at[l], mv_sem.at[u, j])
+            store.start()
+            stores.append(store)
+    for keep in kept:
+        keep.wait()
+    for phase in range(3):
+        for u, (i, l) in enumerate(units):
+            for k, cols in enumerate(widths(shapes[i][2], u)):
+                ici(u, k, phase, i, l, cols).wait_recv()
+                follow = [d2d(u, k, phase + 1, i, l, cols)]
+                if phase < 2:
+                    follow.insert(0, ici(u, k, phase + 1, i, l, cols))
+                for copy in follow:
+                    copy.start()
+                    moved.append(copy)
+    for u, (i, l) in enumerate(units):
+        for k, cols in enumerate(widths(shapes[i][2], u)):
+            for piece in range(4):
+                d2d(u, k, piece, i, l, cols).wait_recv()
+    for copy in moved + sends:
+        copy.wait_send()
+    for store in stores:
+        store.wait()
+
+
+def step_and_gather(sq, g, w, m, v, count):
+    shapes = [t.shape for t in m]
+    n_units = sum(s[0] for s in shapes)
+    blocks = [t.reshape(t.shape[0], 16, -1, t.shape[2]) for t in w]
+    vmem, hbm = pl.BlockSpec(memory_space=pltpu.VMEM), pl.BlockSpec(memory_space=pl.ANY)
+    dma = pltpu.SemaphoreType.DMA
+    out = pl.pallas_call(
+        functools.partial(gather_kernel, shapes, count),
+        out_shape=[jax.ShapeDtypeStruct((s[0], 2, 2, 2, 2) + s[1:], jnp.bfloat16) for s in shapes]
+        + [jax.ShapeDtypeStruct(s, jnp.float32) for s in shapes] * 2,
+        in_specs=[vmem] + [vmem] * 3 + [hbm] * 3 + [vmem] * 6,
+        out_specs=[hbm] * 9,
+        scratch_shapes=[pltpu.VMEM(s, jnp.bfloat16) for s in shapes] * 2
+        + [pltpu.VMEM(s, jnp.float32) for s in shapes] * 2
+        + [
+            pltpu.VMEM((16, 8, 128), jnp.float32),
+            dma((16,)),
+            dma((16,)),
+            dma((n_units,)),
+            dma((n_units,)),
+            dma((n_units, 2)),
+            dma((3 * n_units, 3)),
+            dma((3 * n_units, 3)),
+            dma((3 * n_units, 4)),
+            dma((3 * n_units, 4)),
+        ],
+        compiler_params=pltpu.CompilerParams(collective_id=0, has_side_effects=True, vmem_limit_bytes=60 * 2**20),
+        name="step_and_gather",
+    )(sq, *g, *blocks, *m, *v)
+    return [t.reshape(old.shape) for t, old in zip(out[:3], w)] + list(out[3:])
 
 
 def solution(mesh):
@@ -57,18 +209,9 @@
                 back = da * scale - wide * (scale**3 * jnp.mean(da * wide, -1, keepdims=True))
                 d = d + back.astype(jnp.bfloat16)
 
-        g = [[t.astype(jnp.float32) for t in shards[name]] for name in NAMES]
-        total = lax.psum(sum(jnp.sum(t * t) for ts in g for t in ts), "dp")
-        count = sum(t.size for ts in g for t in ts) * n
-        factor = jnp.minimum(1.0, 0.5 * lax.rsqrt(total / count + 1e-30))
-        me = lax.axis_index("dp")
-        new = []
-        for w, mm, vv, ts in zip((w_gate, w_up, w_down), m, v, g, strict=True):
-            rows = mm.shape[1]
-            own = lax.dynamic_slice_in_dim(w, me * rows, rows, 1).astype(jnp.float32)
-            nw, nm, nv = adamw(own, mm, vv, jnp.stack(ts) * factor)
-            new.append((lax.all_gather(nw, "dp", axis=1, tiled=True), nm, nv))
-        return tuple(one[which] for which in range(3) for one in new)
+        g = [jnp.stack(shards[name]) for name in NAMES]
+        part = sum(jnp.sum(jnp.square(t.astype(jnp.float32)).reshape(-1, 8, 128), axis=0) for t in g)
+        return tuple(step_and_gather(part, g, (w_gate, w_up, w_down), m, v, sum(t.size for t in g) * n))
 
     seq, whole, rows = P(("rep", "dp"), None, None), P(), P(None, "dp", None)
     return jax.shard_map(

time: 890 us -> 807 us (0.907)
  waiting for transfers between devices: 431 us -> 262 us
  Pallas kernels: 0 us -> 129 us
  blocking collectives: 33.3 us -> 0 us
  other arithmetic: 36.2 us -> 21.4 us
    all_gather x3 -> x0, waiting for transfers between devices: 173 us -> none  [step(): new.append((lax.all_gather(nw, 'dp', axis=1, tiled=True), nm, nv))]
    pallas_call x0 -> x1, Pallas kernels: none -> 129 us  [step_and_gather(): pl.pallas_call(functools.partial(gather_kernel, shapes, count), out_shape...]
    psum x1 -> x0, blocking collectives: 33.3 us -> none  [step(): total = lax.psum(sum((jnp.sum(t * t) for ts in g for t in ts)), 'dp')]
    convert_element_type x3 -> x0, other arithmetic: 11 us -> none  [adamw(): return ((w - 0.02 * step).astype(jnp.bfloat16), m, v)]
    unnamed x43 -> x47, local copies, waits for them, and re-layouts: 37.5 us -> 44.6 us
  transfers between devices with their start and end apart: 9 -> 6, of which waited for: 7 -> 4; matrix products, arithmetic and copies ran while one was open for 23% -> 23% of each run, Pallas kernels for 0% -> 0%
where the time goes in v2:
time: 807 us; the launch traced here: 800 us
  matrix products  326 us (40%)
  waiting for transfers between devices  262 us (32%)
  Pallas kernels  129 us (16%)
  local copies, waits for them, and re-layouts  45.9 us (6%)
  other arithmetic  21.4 us (3%)
  between operations  14.8 us (2%)
    dot_general x15, matrix products, dot(): lax.dot_general(a, b, (dims, ((), ())), preferred_element_type=jnp.float32)  326 us
    reduce_scatter x6, waiting for transfers between devices, scatter(): lax.psum_scatter(t.astype(jnp.bfloat16), 'dp', scatter_dimension=0, tiled...  262 us
    pallas_call x1, Pallas kernels, step_and_gather(): pl.pallas_call(functools.partial(gather_kernel, shapes, count), out_shape...  129 us
    unnamed x47, local copies, waits for them, and re-layouts  44.6 us
  transfers between devices with their start and end apart: 6, of which 4 were waited for; matrix products, arithmetic and copies ran while one was open for 23% of the time, Pallas kernels for 0%

profile of v2, /device:TPU:0, one launch (start us, length us, event | category | flops | bytes accessed | tf_op | source)
XLA Modules:
  0.0 799.8 jit_solution(11420203937476506443)
XLA Ops:
  7.2 6.5 copy.20
  13.7 3.1 fusion.13
  16.8 19.9 %fusion.33 = f32[2048,2816]{1,0:T(8,128)} fusion(bf16[2,1024,2816]{2,1,0:T(8,128)(2,1)} %param.13, bf16[1,2048,1024]{2,1,0:T(8,128)(2,1)} %param.11, f32[2048]{0:T(1024)S(1)} %add_rsqrt_fusion.1), kind=kOutput, calls=%fused_computation.48 | convolution fusion | flops 11817451520 | bytes 33038336 | tf_op jit(solution)/shard_map/dot_general | solution.py:16
  36.7 28.7 %multiply_convert_fusion.1 = (bf16[2048,2816]{1,0:T(8,128)(2,1)}, f32[2048,2816]{1,0:T(8,128)}) fusion(f32[2048,2816]{1,0:T(8,128)} %fusion.33, bf16[2,1024,2816]{2,1,0:T(8,128)(2,1)} %param.14, bf16[1,2048,1024]{2,1,0:T(8,128)(2,1)} %param.11, f32[2048]{0:T(1024)S(1)} %add_rsqrt_fusion.1), kind=kOutput, calls=%fused_computation.13 | convolution fusion | flops 11852054528 | bytes 67641344 | tf_op jit(solution)/shard_map/dot_general | solution.py:16
  65.4 19.6 %fusion.15 = (f32[2048]{0:T(1024)S(1)}, bf16[2048,1024]{0,1:T(8,128)(2,1)}) fusion(bf16[2048,2816]{1,0:T(8,128)(2,1)} %get-tuple-element.29, bf16[2,2816,1024]{2,1,0:T(8,128)(2,1)} %param.15, bf16[1,2048,1024]{1,2,0:T(8,128)(2,1)} %copy.20), kind=kOutput, calls=%fused_computation.29 | convolution fusion | flops 11821643776 | bytes 25698304 | tf_op jit(solution)/shard_map/dot_general | solution.py:16
  85.0 20.2 %fusion.26 = f32[2048,2816]{1,0:T(8,128)} fusion(bf16[2,1024,2816]{2,1,0:T(8,128)(2,1)} %param.14, bf16[2048,1024]{0,1:T(8,128)(2,1)} %get-tuple-element.32, f32[2048]{0:T(1024)S(1)} %add_rsqrt_fusion), kind=kOutput, calls=%fused_computation.41 | convolution fusion | flops 11817451520 | bytes 33038336 | tf_op jit(solution)/shard_map/dot_general | solution.py:16
  105.2 18.1 %fusion.22 = f32[2048,2816]{1,0:T(8,128)} fusion(bf16[2,1024,2816]{2,1,0:T(8,128)(2,1)} %param.13, bf16[2048,1024]{0,1:T(8,128)(2,1)S(1)} %copy-done.4, f32[2048]{0:T(1024)S(1)} %add_rsqrt_fusion), kind=kOutput, calls=%fused_computation.37 | convolution fusion | flops 11817451520 | bytes 33038336 | tf_op jit(solution)/shard_map/dot_general | solution.py:16
  123.3 33.9 %fusion.2 = (bf16[2048,2816]{1,0:T(8,128)(2,1)}, bf16[2048,2816]{1,0:T(8,128)(2,1)}) fusion(f32[2048,2816]{1,0:T(8,128)} %fusion.22, f32[2048,2816]{1,0:T(8,128)} %fusion.26, bf16[2,2816,1024]{2,1,0:T(8,128)(2,1)} %param.15, bf16[1,2048,1024]{2,1,0:T(8,128)(2,1)} %param.12), kind=kOutput, calls=%fused_computation.6 | convolution fusion | flops 11897667584 | bytes 79167488 | tf_op jit(solution)/shard_map/dot_general | solution.py:16
  157.2 18.5 %convolution_convert_fusion.4 = bf16[1024,2816]{1,0:T(8,128)(2,1)} fusion(bf16[2048,2816]{1,0:T(8,128)(2,1)} %get-tuple-element.28, bf16[2048,1024]{0,1:T(8,128)(2,1)} %get-tuple-element.32, f32[2048]{0:T(1024)S(1)} %add_rsqrt_fusion), kind=kOutput, calls=%fused_computation.59 | convolution fusion | flops 11820335104 | bytes 21504000 | tf_op jit(solution)/shard_map/dot_general | solution.py:16
  175.8 0.0 reduce-scatter.7.cloned.1.call-start
  175.8 19.2 %fusion.20 = f32[2048,1024]{0,1:T(8,128)} fusion(bf16[2048,2816]{1,0:T(8,128)(2,1)} %get-tuple-element.28, bf16[2,1024,2816]{2,1,0:T(8,128)(2,1)} %param.13), kind=kOutput, calls=%fused_computation.35 | convolution fusion | flops 11811160064 | bytes 25690112 | tf_op jit(solution)/shard_map/dot_general | solution.py:16
  195.0 6.5 copy.21
  201.5 21.2 %fusion.17 = (f32[2048]{0:T(1024)S(1)}, f32[2048,1024]{0,1:T(8,128)}) fusion(bf16[2048,1024]{0,1:T(8,128)(2,1)} %get-tuple-element.32, f32[2048,1024]{0,1:T(8,128)} %fusion.20, bf16[2048,2816]{1,0:T(8,128)(2,1)} %get-tuple-element.27, bf16[2,1024,2816]{2,1,0:T(8,128)(2,1)} %param.14), kind=kOutput, calls=%fused_computation.31 | convolution fusion | flops 11819546624 | bytes 38281216 | tf_op jit(solution)/shard_map/dot_general | solution.py:16
  222.7 5.9 fusion.56
  228.7 18.8 %convolution_convert_fusion = bf16[2048,2816]{1,0:T(8,128)(2,1)} fusion(bf16[2048,1024]{0,1:T(8,128)(2,1)S(1)} %fusion.56, bf16[2,2816,1024]{2,1,0:T(8,128)(2,1)} %param.15), kind=kOutput, calls=%fused_computation.23 | convolution fusion | flops 11816927232 | bytes 21495808 | tf_op jit(solution)/shard_map/dot_general | solution.py:16
  247.5 25.0 %fusion.40 = bf16[1024,2816]{1,0:T(8,128)(2,1)} fusion(f32[2048,2816]{1,0:T(8,128)} %get-tuple-element.30, bf16[2048,2816]{1,0:T(8,128)(2,1)} %convolution_convert_fusion, f32[2048,2816]{1,0:T(8,128)} %fusion.33, bf16[1,2048,1024]{1,2,0:T(8,128)(2,1)S(1)} %copy-done, f32[2048]{0:T(1024)S(1)} %copy-done.14), kind=kOutput, calls=%fused_computation.55 | convolution fusion | flops 11883773952 | bytes 67641344 | tf_op jit(solution)/shard_map/dot_general | solution.py:16
  272.5 18.6 %convolution_convert_fusion.3 = bf16[1024,2816]{1,0:T(8,128)(2,1)} fusion(bf16[2048,2816]{1,0:T(8,128)(2,1)} %get-tuple-element.27, bf16[2048,1024]{0,1:T(8,128)(2,1)} %get-tuple-element.32, f32[2048]{0:T(1024)S(1)} %add_rsqrt_fusion), kind=kOutput, calls=%fused_computation.58 | convolution fusion | flops 11820335104 | bytes 21504000 | tf_op jit(solution)/shard_map/dot_general | solution.py:16
  291.1 0.0 reduce-scatter.11.cloned.1.call-start
  291.2 22.9 %fusion.43 = bf16[1024,2816]{1,0:T(8,128)(2,1)} fusion(bf16[2048,2816]{1,0:T(8,128)(2,1)} %convolution_convert_fusion, f32[2048,2816]{1,0:T(8,128)} %fusion.33, bf16[1,2048,1024]{1,2,0:T(8,128)(2,1)} %copy.20, f32[2048]{0:T(1024)S(1)} %copy-done.14), kind=kOutput, calls=%fused_computation.56 | convolution fusion | flops 11860705280 | bytes 44572672 | tf_op jit(solution)/shard_map/dot_general | solution.py:16
  314.1 23.4 %fusion.39 = bf16[2816,1024]{1,0:T(8,128)(2,1)} fusion(f32[2048,2816]{1,0:T(8,128)} %fusion.26, bf16[1,2048,1024]{2,1,0:T(8,128)(2,1)} %param.12, f32[2048,2816]{1,0:T(8,128)} %fusion.22), kind=kOutput, calls=%fused_computation.54 | convolution fusion | flops 11848646656 | bytes 56098816 | tf_op jit(solution)/shard_map/dot_general | solution.py:16
  337.6 18.4 %convolution_convert_fusion.2 = bf16[2816,1024]{1,0:T(8,128)(2,1)} fusion(bf16[2048,2816]{1,0:T(8,128)(2,1)} %get-tuple-element.29, bf16[2048,1024]{0,1:T(8,128)(2,1)} %copy-done.3), kind=kOutput, calls=%fused_computation.57 | convolution fusion | flops 11814043648 | bytes 21495808 | tf_op jit(solution)/shard_map/dot_general | solution.py:16
  356.1 2.0 pad_maximum_fusion.refs_0_
  358.2 55.1 %reduce-scatter.13.cloned.1.call-done = bf16[64,2816]{1,0:T(8,128)(2,1)} async-done(((bf16[1024,2816]{1,0:T(8,128)(2,1)}), bf16[64,2816]{1,0:T(8,128)(2,1)}) %reduce-scatter.13.cloned.1.call-update) | async-done | bytes 360464 | tf_op jit(solution)/shard_map/reduce_scatter | solution.py:194
  413.2 70.2 %reduce-scatter.11.cloned.1.call-done = bf16[64,2816]{1,0:T(8,128)(2,1)} async-done(((bf16[1024,2816]{1,0:T(8,128)(2,1)}), bf16[64,2816]{1,0:T(8,128)(2,1)}) %reduce-scatter.11.cloned.1.call-update) | async-done | bytes 360464 | tf_op jit(solution)/shard_map/reduce_scatter | solution.py:194
  483.4 2.0 pad_maximum_fusion.1.refs_1_
  485.4 1.2 convert_multiply_fusion.11
  486.6 1.2 convert_multiply_fusion.10
  487.8 66.8 %reduce-scatter.17.cloned.1.call-done = bf16[176,1024]{1,0:T(8,128)(2,1)} async-done(((bf16[2816,1024]{1,0:T(8,128)(2,1)}), bf16[176,1024]{1,0:T(8,128)(2,1)}) %reduce-scatter.17.cloned.1.call-update) | async-done | bytes 360464 | tf_op jit(solution)/shard_map/reduce_scatter | solution.py:194
  554.6 70.2 %reduce-scatter.15.cloned.1.call-done = bf16[176,1024]{1,0:T(8,128)(2,1)} async-done(((bf16[2816,1024]{1,0:T(8,128)(2,1)}), bf16[176,1024]{1,0:T(8,128)(2,1)}) %reduce-scatter.15.cloned.1.call-update) | async-done | bytes 360464 | tf_op jit(solution)/shard_map/reduce_scatter | solution.py:194
  624.8 1.3 multiply_reduce_fusion
  626.0 2.0 pad_maximum_fusion.2.refs_2_
  628.0 1.2 square.20
  629.2 0.1 square.22
  629.3 1.7 reduce_sum.59
  631.1 0.4 reduce_sum.60
  631.4 0.6 bitcast_add_fusion.1.sq
  632.0 128.8 %step_and_gather.1 = (bf16[2,2,2,2,2,64,2816]{6,5,4,3,2,1,0:T(8,128)(2,1)}, bf16[2,2,2,2,2,64,2816]{6,5,4,3,2,1,0:T(8,128)(2,1)}, bf16[2,2,2,2,2,176,1024]{6,5,4...) custom-call(f32[8,128]{1,0:T(8,128)} %bitcast_add_fusion.1.sq, ...), custom_call_target="tpu_custom_call" | custom-call | tf_op jit(solution)/shard_map/step_and_gather/pallas_call | solution.py:146
  760.9 11.7 %copy.31 = bf16[2,1024,2816]{2,1,0:T(8,128)(2,1)} copy(bf16[2,1024,2816]{2,1,0:T(8,128)(2,1)} %bitcast.84) | data formatting | bytes 23068672
  772.6 5.8 copy.32
  778.4 0.7 slice-done.1
  779.1 1.3 slice-done.2
  780.4 5.4 copy.33
  785.8 1.1 copy.34
  786.9 1.1 copy.35
  788.0 1.1 copy.36
  789.1 1.1 copy.37
  790.2 1.1 copy.38
  791.3 1.1 copy.39
  (50 shorter events, 0.4 us)
Async XLA Ops:
  7.2 348.9 %reduce-scatter.9.cloned.1.call-start = ((), (), s32[]{:S(2)}) async-start(), calls=%async_computation.7 | async-start | bytes 6127616 | tf_op jit(solution)/shard_map/reduce_scatter | solution.py:194
  16.8 19.9 %copy-start.13 = (f32[2048]{0:T(1024)}, f32[2048]{0:T(1024)S(1)}, u32[]{:S(2)}) copy-start(f32[2048]{0:T(1024)S(1)} %add_rsqrt_fusion.1) | copy-start | bytes 24580
  85.0 20.3 %copy-start.11 = (f32[2048]{0:T(1024)}, f32[2048]{0:T(1024)S(1)}, u32[]{:S(2)}) copy-start(f32[2048]{0:T(1024)S(1)} %get-tuple-element.31) | copy-start | bytes 24580
  85.0 20.2 %copy-start.4 = (bf16[2048,1024]{0,1:T(8,128)(2,1)S(1)}, bf16[2048,1024]{0,1:T(8,128)(2,1)}, u32[]{:S(2)}) copy-start(bf16[2048,1024]{0,1:T(8,128)(2,1)} %get-tuple-element.32) | copy-start | bytes 12582916
  175.8 180.4 %reduce-scatter.7.cloned.1.call-start = ((), (), s32[]{:S(2)}) async-start(), calls=%async_computation.6 | async-start | bytes 6127616 | tf_op jit(solution)/shard_map/reduce_scatter | solution.py:194
  201.5 21.2 %copy-start.12 = (f32[2048]{0:T(1024)S(1)}, f32[2048]{0:T(1024)}, u32[]{:S(2)}) copy-start(f32[2048]{0:T(1024)} %copy-done.11) | copy-start | bytes 24580
  201.5 21.2 %copy-start.1 = (bf16[1,2048,1024]{1,2,0:T(8,128)(2,1)S(1)}, bf16[1,2048,1024]{1,2,0:T(8,128)(2,1)}, u32[]{:S(2)}) copy-start(bf16[1,2048,1024]{1,2,0:T(8,128)(2,1)} %copy.21) | copy-start | bytes 12582916
  228.7 18.8 %copy-start.3 = (bf16[2048,1024]{0,1:T(8,128)(2,1)}, bf16[2048,1024]{0,1:T(8,128)(2,1)S(1)}, u32[]{:S(2)}) copy-start(bf16[2048,1024]{0,1:T(8,128)(2,1)S(1)} %fusion.56) | copy-start | bytes 12582916
  228.7 18.8 %copy-start = (bf16[1,2048,1024]{1,2,0:T(8,128)(2,1)S(1)}, bf16[1,2048,1024]{1,2,0:T(8,128)(2,1)}, u32[]{:S(2)}) copy-start(bf16[1,2048,1024]{1,2,0:T(8,128)(2,1)} %copy.20) | copy-start | bytes 12582916
  228.7 18.8 %copy-start.14 = (f32[2048]{0:T(1024)S(1)}, f32[2048]{0:T(1024)}, u32[]{:S(2)}) copy-start(f32[2048]{0:T(1024)} %copy-done.13) | copy-start | bytes 24580
  272.5 140.8 %reduce-scatter.13.cloned.1.call-start = ((), (), s32[]{:S(2)}) async-start(), calls=%async_computation.9 | async-start | bytes 6127616 | tf_op jit(solution)/shard_map/reduce_scatter | solution.py:194
  291.1 192.3 %reduce-scatter.11.cloned.1.call-start = ((), (), s32[]{:S(2)}) async-start(), calls=%async_computation.8 | async-start | bytes 6127616 | tf_op jit(solution)/shard_map/reduce_scatter | solution.py:194
  314.0 240.6 %reduce-scatter.17.cloned.1.call-start = ((), (), s32[]{:S(2)}) async-start(), calls=%async_computation.11 | async-start | bytes 6127616 | tf_op jit(solution)/shard_map/reduce_scatter | solution.py:194
  337.6 287.2 %reduce-scatter.15.cloned.1.call-start = ((), (), s32[]{:S(2)}) async-start(), calls=%async_computation.10 | async-start | bytes 6127616 | tf_op jit(solution)/shard_map/reduce_scatter | solution.py:194
  760.8 11.7 %copy-start.2 = (bf16[2,2,2,2,2,64,2816]{6,5,4,3,2,1,0:T(8,128)(2,1)S(1)}, bf16[2,2,2,2,2,64,2816]{6,5,4,3,2,1,0:T(8,128)(2,1)}, u32[]{:S(2)}) copy-start(bf16[2,2,2,2,2,64,2816]{6,5,4,3,2,1,0:T(8,128)(2,1)} %get-tuple-element.19) | copy-start | bytes 34603012
  760.9 17.6 %slice-start = ((s8[11534336]{0:T(1024)(128)(4,1)}), s8[4194304]{0:T(1024)(128)(4,1)S(1)}, s32[]{:S(2)}) async-start(s8[11534336]{0:T(1024)(128)(4,1)} %bitcast.80), calls=%async_computation.12 | async-start | bytes 8388608
  760.9 18.2 %slice-start.1 = ((s8[11534336]{0:T(1024)(128)(4,1)}), s8[4194304]{0:T(1024)(128)(4,1)S(1)}, s32[]{:S(2)}) async-start(s8[11534336]{0:T(1024)(128)(4,1)} %bitcast.80), calls=%async_computation.13 | async-start | bytes 8388608
  772.6 7.8 slice-start.2
  780.4 5.4 copy-start.10
  780.4 6.5 copy-start.9
  780.4 7.6 copy-start.8
  785.8 3.3 copy-start.7
  785.8 4.4 copy-start.6
  785.8 5.5 copy-start.5
Sparse Core Ops, SparseCore 0:
  175.9 70.5 reduce-scatter.8
  272.6 70.3 reduce-scatter.6
  345.3 67.9 reduce-scatter.12
  415.4 67.9 reduce-scatter.10
  486.1 68.4 reduce-scatter.16
  557.3 67.3 reduce-scatter.14

commit v3 on v2

--- a/solution.py
+++ b/solution.py
@@ -31,9 +31,10 @@
 
 
 def gather_kernel(shapes, count, sq, *refs):
-    n_mat = len(shapes)
-    g, w, m, v, new_w, new_m, new_v, own_w, out_w, out_m, out_v = (refs[i * n_mat : (i + 1) * n_mat] for i in range(11))
-    squares, sq_send, sq_recv, in_sem, keep_sem, mv_sem, ici_send, ici_recv, d2d_send, d2d_recv = refs[11 * n_mat :]
+    n_mat, layers, ff = len(shapes), shapes[0][0], shapes[0][2]
+    gu, dn, refs = refs[:layers], refs[layers : 2 * layers], refs[2 * layers :]
+    w, m, v, new_w, new_m, new_v, own_w, out_w, out_m, out_v = (refs[i * n_mat : (i + 1) * n_mat] for i in range(10))
+    squares, sq_send, sq_recv, in_sem, keep_sem, mv_sem, ici_send, ici_recv, d2d_send, d2d_recv = refs[10 * n_mat :]
     me = lax.axis_index("dp")
     at = [(me // s) % 2 for s in LINKS]
     core = me % 2
@@ -97,7 +98,8 @@
     moved, kept, stores = [], [], []
     for u, (i, l) in enumerate(units):
         loads[u].wait()
-        clipped = g[i][l].astype(jnp.float32) * factor
+        g = dn[l][...] if i == 2 else gu[l][:, i * ff : (i + 1) * ff]
+        clipped = g.astype(jnp.float32) * factor
         mm = 0.9 * m[i][l] + 0.1 * clipped
         vv = 0.95 * v[i][l] + 0.05 * clipped * clipped
         old = own_w[i][l].astype(jnp.float32)
@@ -137,7 +139,7 @@
         store.wait()
 
 
-def step_and_gather(sq, g, w, m, v, count):
+def step_and_gather(sq, gu, dn, w, m, v, count):
     shapes = [t.shape for t in m]
     n_units = sum(s[0] for s in shapes)
     blocks = [t.reshape(t.shape[0], 16, -1, t.shape[2]) for t in w]
@@ -147,7 +149,7 @@
         functools.partial(gather_kernel, shapes, count),
         out_shape=[jax.ShapeDtypeStruct((s[0], 2, 2, 2, 2) + s[1:], jnp.bfloat16) for s in shapes]
         + [jax.ShapeDtypeStruct(s, jnp.float32) for s in shapes] * 2,
-        in_specs=[vmem] + [vmem] * 3 + [hbm] * 3 + [vmem] * 6,
+        in_specs=[vmem] * (1 + len(gu) + len(dn)) + [hbm] * 3 + [vmem] * 6,
         out_specs=[hbm] * 9,
         scratch_shapes=[pltpu.VMEM(s, jnp.bfloat16) for s in shapes] * 2
         + [pltpu.VMEM(s, jnp.float32) for s in shapes] * 2
@@ -165,8 +167,229 @@
         ],
         compiler_params=pltpu.CompilerParams(collective_id=0, has_side_effects=True, vmem_limit_bytes=60 * 2**20),
         name="step_and_gather",
-    )(sq, *g, *blocks, *m, *v)
+    )(sq, *gu, *dn, *blocks, *m, *v)
     return [t.reshape(old.shape) for t, old in zip(out[:3], w)] + list(out[3:])
+
+
+UNIT = 256
+LAGS = (2, 5, 8, 11)
+DOWN_STEPS = (3, 9, 14, 18)
+
+
+def fold(t):
+    t = jnp.sum(jnp.square(t).reshape(-1, 8, t.shape[-1]), axis=0)
+    return sum(t[:, j : j + 128] for j in range(0, t.shape[-1], 128))
+
+
+def reduce_kernel(per, with_da, *refs):
+    a_t, down, dgate, dup, *refs = refs
+    if with_da:
+        w_gate, w_up, *refs = refs
+    gu, dn, sq, *refs = refs
+    if with_da:
+        da, *refs = refs
+    tile, got, kept1, kept2, kept3, out1, out2, out3, in1, in2, in3 = refs[:11]
+    d_own, d_got, d_kept1, d_kept2, d_kept3, d_out1, d_out2, d_out3, d_in1, d_in2, d_in3 = refs[11:22]
+    stream, w_stream, s_sem, w_sem, send, recv, d_send, d_recv, own_sem = refs[22:]
+    kept, outs, ins = (kept1, kept2, kept3), (out1, out2, out3), (in1, in2, in3)
+    d_kept, d_outs, d_ins = (d_kept1, d_kept2, d_kept3), (d_out1, d_out2, d_out3), (d_in1, d_in2, d_in3)
+    n_units = 2 * per
+    me = lax.axis_index("dp")
+    at = [(me // s) % 2 for s in LINKS]
+    core = me % 2
+    everything = slice(None)
+
+    def remote(src, dst, s, r, stride):
+        return pltpu.make_async_remote_copy(src, dst, s, r, device_id={"dp": flipped(me, stride)}, device_id_type=MESH)
+
+    def hop(u, k, stage):
+        if stage == 0:
+            return remote(tile.at[u % 3, :, :, :, 1 - core], got.at[u], send.at[0, u], recv.at[0, u], 1)
+        return remote(outs[stage - 1].at[u], ins[stage - 1].at[u], send.at[stage, u], recv.at[stage, u], LINKS[(k + stage - 1) % 3])
+
+    def down_hop(k, stage):
+        cols = pl.ds(*widths(dn.shape[1], 0)[k])
+        if stage == 0:
+            src, dst, stride = down.at[:, :, :, 1 - core, :, cols], d_got.at[:, :, :, :, cols], 1
+        else:
+            lead = (everything,) * (4 - stage)
+            src, dst = d_outs[stage - 1].at[(*lead, cols)], d_ins[stage - 1].at[(*lead, cols)]
+            stride = LINKS[(k + stage - 1) % 3]
+        return remote(src, dst, d_send.at[stage, k], d_recv.at[stage, k], stride)
+
+    def halves(k, stage):
+        axes = [d for d in range(3) if d not in [(k + j) % 3 for j in range(stage - 1)]]
+        d = (k + stage - 1) % 3
+        return [tuple(side if axis == d else everything for axis in axes) for side in (1 - at[d], at[d])]
+
+    def add_up(u, k, stage):
+        hop(u, k, stage - 1).wait_recv()
+        if stage == 1:
+            hop(u, k, 0).wait_send()
+
+        def total(where):
+            if stage == 1:
+                mine, other = tile[(u % 3, *where, core)], got[(u, *where)]
+            else:
+                mine, other = kept[stage - 2][(u % 4, *where)], ins[stage - 2][(u, *where)]
+            return mine.astype(jnp.float32) + other.astype(jnp.float32)
+
+        if stage == 4:
+            g = total(()).astype(jnp.bfloat16)
+            gu[:, pl.ds(pl.multiple_of(u * UNIT, UNIT), UNIT)] = g
+            sq[...] += fold(g.astype(jnp.float32))
+            return
+        away, here = halves(k, stage)
+        outs[stage - 1][u] = total(away).astype(jnp.bfloat16)
+        hop(u, k, stage).start()
+        kept[stage - 1][u % 4] = total(here)
+
+    def add_down(k, stage):
+        down_hop(k, stage - 1).wait_recv()
+        cols = pl.ds(*widths(dn.shape[1], 0)[k])
+
+        def total(where):
+            mine, other = (d_own, d_got) if stage == 1 else (d_kept[stage - 2], d_ins[stage - 2])
+            at_ = (*where, everything, cols)
+            return mine[at_].astype(jnp.float32) + other[at_].astype(jnp.float32)
+
+        if stage == 4:
+            g = total(()).astype(jnp.bfloat16)
+            dn[:, cols] = g
+            sq[...] += fold(g.astype(jnp.float32))
+            return
+        away, here = halves(k, stage)
+        rest = (everything,) * (4 - stage)
+        d_outs[stage - 1][(*rest, cols)] = total(away).astype(jnp.bfloat16)
+        down_hop(k, stage).start()
+        d_kept[stage - 1][(*rest, cols)] = total(here)
+
+    def loads(u, arrays):
+        col = pl.ds(pl.multiple_of((u % per) * UNIT, UNIT), UNIT)
+        slot = u % 2
+        pairs = [(arrays[0], stream, s_sem)] + ([(arrays[1], w_stream, w_sem)] if with_da else [])
+        return [pltpu.make_async_copy(src.at[:, col], dst.at[slot], sem.at[slot]) for src, dst, sem in pairs]
+
+    def load(u):
+        for which in range(2):
+
+            @pl.when(u // per == which)
+            def _():
+                for copy in loads(u, ((dgate, dup)[which], (w_gate, w_up)[which] if with_da else None)):
+                    copy.start()
+
+    own = pltpu.make_async_copy(down.at[:, :, :, core], d_own, own_sem)
+    own.start()
+    load(0)
+    barrier = pltpu.get_barrier_semaphore()
+    for stride in (1, *LINKS):
+        pl.semaphore_signal(barrier, inc=1, device_id={"dp": flipped(me, stride)}, device_id_type=MESH)
+    pl.semaphore_wait(barrier, 4)
+    for k in range(3):
+        down_hop(k, 0).start()
+    sq[...] = jnp.zeros_like(sq)
+    if with_da:
+        da[...] = jnp.zeros_like(da)
+    own.wait()
+
+    def step(t, _):
+        @pl.when(t + 1 < n_units)
+        def _():
+            load(t + 1)
+
+        for stage, lag in reversed(list(enumerate(LAGS, 1))):
+            u = t - lag
+            for k in range(3):
+
+                @pl.when((u >= 0) & (u < n_units) & ((u + 33) % 3 == k))
+                def _():
+                    add_up(u, k, stage)
+
+        for stage, when in enumerate(DOWN_STEPS, 1):
+
+            @pl.when(t == when)
+            def _():
+                for k in range(3):
+                    add_down(k, stage)
+
+        @pl.when(t < n_units)
+        def _():
+            for copy in loads(t, (dgate, w_gate if with_da else None)):
+                copy.wait()
+            slot = t % 2
+            g = jnp.dot(a_t[...], stream[slot], preferred_element_type=jnp.float32).astype(jnp.bfloat16)
+            tile[t % 3] = g.reshape(tile.shape[1:])
+            hop(t, 0, 0).start()
+            if with_da:
+
+                def rows(j, _):
+                    part = pl.ds(pl.multiple_of(j * 512, 512), 512)
+                    da[part] += lax.dot_general(
+                        stream[slot, part], w_stream[slot], (((1,), (1,)), ((), ())), preferred_element_type=jnp.float32
+                    )
+
+                lax.fori_loop(0, da.shape[0] // 512, rows, None)
+
+    lax.fori_loop(0, n_units + LAGS[-1], step, None)
+
+    def drain(u, _):
+        for stage in (1, 2, 3):
+            hop(u, 0, stage).wait_send()
+
+    lax.fori_loop(0, n_units, drain, None)
+    for k in range(3):
+        for stage in range(4):
+            down_hop(k, stage).wait_send()
+
+
+def reduce_layer(a, down, dgate, dup, weights, collective_id):
+    tokens, d = a.shape
+    ff = dgate.shape[1]
+    per, rows, d_rows, with_da = ff // UNIT, d // 16, ff // 16, weights is not None
+    n_units = 2 * per
+    vmem, hbm = pl.BlockSpec(memory_space=pltpu.VMEM), pl.BlockSpec(memory_space=pl.ANY)
+    dma, b16, f32 = pltpu.SemaphoreType.DMA, jnp.bfloat16, jnp.float32
+    whole = [jax.ShapeDtypeStruct((tokens, d), f32)] if with_da else []
+    return pl.pallas_call(
+        functools.partial(reduce_kernel, per, with_da),
+        out_shape=[
+            jax.ShapeDtypeStruct((rows, 2 * ff), b16),
+            jax.ShapeDtypeStruct((d_rows, d), b16),
+            jax.ShapeDtypeStruct((8, 128), f32),
+        ]
+        + whole,
+        in_specs=[vmem] + [hbm] * (5 if with_da else 3),
+        out_specs=[vmem] * (3 + len(whole)),
+        scratch_shapes=[
+            pltpu.VMEM((3, 2, 2, 2, 2, rows, UNIT), b16),
+            pltpu.VMEM((n_units, 2, 2, 2, rows, UNIT), b16),
+            pltpu.VMEM((4, 2, 2, rows, UNIT), f32),
+            pltpu.VMEM((4, 2, rows, UNIT), f32),
+            pltpu.VMEM((4, rows, UNIT), f32),
+        ]
+        + [
+            pltpu.VMEM((n_units, 2, 2, rows, UNIT), b16),
+            pltpu.VMEM((n_units, 2, rows, UNIT), b16),
+            pltpu.VMEM((n_units, rows, UNIT), b16),
+        ]
+        * 2
+        + [pltpu.VMEM((2, 2, 2, d_rows, d), b16)] * 2
+        + [pltpu.VMEM((2, 2, d_rows, d), f32), pltpu.VMEM((2, d_rows, d), f32), pltpu.VMEM((d_rows, d), f32)]
+        + [pltpu.VMEM((2, 2, d_rows, d), b16), pltpu.VMEM((2, d_rows, d), b16), pltpu.VMEM((d_rows, d), b16)] * 2
+        + [
+            pltpu.VMEM((2, tokens, UNIT), b16),
+            pltpu.VMEM((2, d, UNIT), b16),
+            dma((2,)),
+            dma((2,)),
+            dma((4, n_units)),
+            dma((4, n_units)),
+            dma((4, 3)),
+            dma((4, 3)),
+            dma(()),
+        ],
+        compiler_params=pltpu.CompilerParams(collective_id=collective_id, has_side_effects=True, vmem_limit_bytes=62 * 2**20),
+        name=f"reduce_layer_{collective_id}",
+    )(a.T, down.reshape(2, 2, 2, 2, d_rows, d), dgate, dup, *(weights or ()))
 
 
 def solution(mesh):
@@ -188,30 +411,27 @@
             if l + 1 < layers:
                 h = h + dot(z, w_down[l], ((1,), (0,))).astype(jnp.bfloat16)
         d = dy[0]
-        shards = {name: [None] * layers for name in NAMES}
-
-        def scatter(t):
-            return lax.psum_scatter(t.astype(jnp.bfloat16), "dp", scatter_dimension=0, tiled=True)
-
+        summed, squares = [None] * layers, 0.0
         for l in reversed(range(layers)):
             h, scale, a, gate, up, z = saved[l]
-            shards["w_down"][l] = scatter(dot(z, d, ((0,), (0,))))
+            down = dot(z, d, ((0,), (0,))).astype(jnp.bfloat16)
             dz = dot(d, w_down[l], ((1,), (1,))).astype(jnp.bfloat16).astype(jnp.float32)
             sig = jax.nn.sigmoid(gate)
             silu = gate * sig
             dup = (dz * silu).astype(jnp.bfloat16)
             dgate = (dz * up * (sig * (1 + gate * (1 - sig)))).astype(jnp.bfloat16)
-            shards["w_gate"][l] = scatter(dot(a, dgate, ((0,), (0,))))
-            shards["w_up"][l] = scatter(dot(a, dup, ((0,), (0,))))
+            gu, dn, sq, *da = reduce_layer(a, down, dgate, dup, (w_gate[l], w_up[l]) if l else None, l + 1)
+            summed[l] = (gu, dn)
+            squares = squares + sq
             if l:
-                da = dot(dgate, w_gate[l], ((1,), (1,))) + dot(dup, w_up[l], ((1,), (1,)))
+                da = da[0]
                 wide = h.astype(jnp.float32)
                 back = da * scale - wide * (scale**3 * jnp.mean(da * wide, -1, keepdims=True))
                 d = d + back.astype(jnp.bfloat16)
 
-        g = [jnp.stack(shards[name]) for name in NAMES]
-        part = sum(jnp.sum(jnp.square(t.astype(jnp.float32)).reshape(-1, 8, 128), axis=0) for t in g)
-        return tuple(step_and_gather(part, g, (w_gate, w_up, w_down), m, v, sum(t.size for t in g) * n))
+        gu, dn = zip(*summed, strict=True)
+        count = sum(t.size for t in m) * n
+        return tuple(step_and_gather(squares, gu, dn, (w_gate, w_up, w_down), m, v, count))
 
     seq, whole, rows = P(("rep", "dp"), None, None), P(), P(None, "dp", None)
     return jax.shard_map(

time: 807 us -> 624 us (0.77)
  waiting for transfers between devices: 262 us -> 0 us
  Pallas kernels: 129 us -> 311 us
  matrix products: 326 us -> 216 us
  local copies, waits for them, and re-layouts: 45.9 us -> 62.9 us
  between operations: 14.8 us -> 1.2 us
    reduce_scatter x6 -> x0, waiting for transfers between devices: 262 us -> none  [scatter(): lax.psum_scatter(t.astype(jnp.bfloat16), 'dp', scatter_dimension=0, tiled...]
    pallas_call x0 -> x2, Pallas kernels: none -> 184 us  [reduce_layer(): pl.pallas_call(functools.partial(reduce_kernel, per, with_da), out_shape=...]
    dot_general x15 -> x9, matrix products: 326 us -> 216 us  [dot(): lax.dot_general(a, b, (dims, ((), ())), preferred_element_type=jnp.float32)]
    squeeze x0 -> x1, local copies, waits for them, and re-layouts: none -> 9.27 us  [step(): up = dot(a, w_up[l], ((1,), (0,)))]
    pallas_call x0 -> x1, local copies, waits for them, and re-layouts: none -> 9.13 us  [reduce_layer(): pl.pallas_call(functools.partial(reduce_kernel, per, with_da), out_shape=...]
  transfers between devices with their start and end apart: 6 -> 0, of which waited for: 4 -> 0; matrix products, arithmetic and copies ran while one was open for 23% -> 0% of each run, Pallas kernels for 0% -> 0%
where the time goes in v3:
time: 624 us; the launch traced here: 617 us
  Pallas kernels  311 us (50%)
  matrix products  216 us (35%)
  local copies, waits for them, and re-layouts  62.9 us (10%)
  other arithmetic  25.1 us (4%)
    dot_general x9, matrix products, dot(): lax.dot_general(a, b, (dims, ((), ())), preferred_element_type=jnp.float32)  216 us
    pallas_call x2, Pallas kernels, reduce_layer(): pl.pallas_call(functools.partial(reduce_kernel, per, with_da), out_shape=...  184 us
    pallas_call x1, Pallas kernels, step_and_gather(): pl.pallas_call(functools.partial(gather_kernel, shapes, count), out_shape...  128 us
    unnamed x47, local copies, waits for them, and re-layouts  44.5 us

profile of v3, /device:TPU:0, one launch (start us, length us, event | category | flops | bytes accessed | tf_op | source)
XLA Modules:
  0.0 616.9 jit_solution(8175491540670855987)
XLA Ops:
  0.6 6.5 %copy.20 = bf16[1,2048,1024]{1,2,0:T(8,128)(2,1)} copy(bf16[1,2048,1024]{2,1,0:T(8,128)(2,1)} %param.11) | data formatting | bytes 8388608 | tf_op args[0]
  7.2 3.1 fusion.9
  10.2 0.0 copy-start.10
  10.2 19.9 %fusion.22 = f32[2048,2816]{1,0:T(8,128)} fusion(bf16[2,1024,2816]{2,1,0:T(8,128)(2,1)} %param.13, bf16[1,2048,1024]{2,1,0:T(8,128)(2,1)} %param.11, f32[2048]{0:T(1024)S(1)} %add_rsqrt_fusion.1), kind=kOutput, calls=%fused_computation.39 | convolution fusion | flops 11817451520 | bytes 33038336 | tf_op jit(solution)/shard_map/dot_general | solution.py:16
  30.1 0.0 copy-done.10
  30.1 28.7 %multiply_convert_fusion.1 = (bf16[2048,2816]{1,0:T(8,128)(2,1)}, f32[2048,2816]{1,0:T(8,128)}) fusion(f32[2048,2816]{1,0:T(8,128)} %fusion.22, bf16[2,1024,2816]{2,1,0:T(8,128)(2,1)} %param.14, bf16[1,2048,1024]{2,1,0:T(8,128)(2,1)} %param.11, f32[2048]{0:T(1024)S(1)} %add_rsqrt_fusion.1), kind=kOutput, calls=%fused_computation.13 | convolution fusion | flops 11852054528 | bytes 67641344 | tf_op jit(solution)/shard_map/dot_general | solution.py:16
  58.8 19.6 %fusion.11 = (f32[2048]{0:T(1024)S(1)}, bf16[2048,1024]{0,1:T(8,128)(2,1)}) fusion(bf16[2048,2816]{1,0:T(8,128)(2,1)} %get-tuple-element.45, bf16[2,2816,1024]{2,1,0:T(8,128)(2,1)} %param.15, bf16[1,2048,1024]{1,2,0:T(8,128)(2,1)} %copy.20), kind=kOutput, calls=%fused_computation.27 | convolution fusion | flops 11821643776 | bytes 25698304 | tf_op jit(solution)/shard_map/dot_general | solution.py:16
  78.4 0.0 copy-start.1
  78.4 20.3 %fusion.40 = f32[2048,2816]{1,0:T(8,128)} fusion(bf16[2048,1024]{0,1:T(8,128)(2,1)} %get-tuple-element.48, f32[2048]{0:T(1024)S(1)} %add_rsqrt_fusion, bf16[2,1024,2816]{2,1,0:T(8,128)(2,1)} %param.13), kind=kOutput, calls=%fused_computation.57 | convolution fusion | flops 11817451520 | bytes 33038336 | tf_op jit(solution)/shard_map/dot_general | solution.py:16
  98.7 0.0 copy-done.12
  98.7 0.0 copy-done.1
  98.7 18.1 %fusion.38 = f32[2048,2816]{1,0:T(8,128)} fusion(bf16[2048,1024]{0,1:T(8,128)(2,1)S(1)} %copy-done.1, f32[2048]{0:T(1024)S(1)} %add_rsqrt_fusion, bf16[2,1024,2816]{2,1,0:T(8,128)(2,1)} %param.14), kind=kOutput, calls=%fused_computation.56 | convolution fusion | flops 11817451520 | bytes 33038336 | tf_op jit(solution)/shard_map/dot_general | solution.py:16
  116.8 34.1 %fusion.2 = (bf16[2048,2816]{1,0:T(8,128)(2,1)}, bf16[2048,2816]{1,0:T(8,128)(2,1)}) fusion(f32[2048,2816]{1,0:T(8,128)} %fusion.40, f32[2048,2816]{1,0:T(8,128)} %fusion.38, bf16[2,2816,1024]{2,1,0:T(8,128)(2,1)} %param.15, bf16[1,2048,1024]{2,1,0:T(8,128)(2,1)} %param.12), kind=kOutput, calls=%fused_computation.6 | convolution fusion | flops 11897667584 | bytes 79167488 | tf_op jit(solution)/shard_map/dot_general | solution.py:16
  150.9 23.6 %fusion.27 = bf16[2816,1024]{1,0:T(8,128)(2,1)} fusion(f32[2048,2816]{1,0:T(8,128)} %fusion.38, bf16[1,2048,1024]{2,1,0:T(8,128)(2,1)} %param.12, f32[2048,2816]{1,0:T(8,128)} %fusion.40), kind=kOutput, calls=%fused_computation.46 | convolution fusion | flops 11848646656 | bytes 56098816 | tf_op jit(solution)/shard_map/dot_general | solution.py:16
  174.5 0.0 copy-done.2
  174.5 3.1 fusion.42.refs_0_
  177.6 9.3 %slice_bitcast_fusion = (bf16[1024,2816]{1,0:T(8,128)(2,1)}, bf16[1024,2816]{1,0:T(8,128)(2,1)}) fusion(bf16[2,1024,2816]{2,1,0:T(8,128)(2,1)} %param.14, bf16[2,1024,2816]{2,1,0:T(8,128)(2,1)} %param.13), kind=kLoop, calls=%fused_computation.42 | loop fusion | bytes 23068672 | tf_op jit(solution)/shard_map/squeeze | solution.py:408
  186.9 105.3 %reduce_layer_2.1 = (bf16[64,5632]{1,0:T(8,128)(2,1)}, bf16[176,1024]{1,0:T(8,128)(2,1)}, f32[8,128]{1,0:T(8,128)}, f32[2048,1024]{1,0:T(8,128)}) custom-call(bf16[1024,2048]{1,0:T(8,128)(2,1)} %fusion.42.refs_0_, bf16[2,2,2,2,176,1024]{5,4,3,2,1,0:T(8,128)(2,1)} %bitcast.74, bf16[2048,2816]{1,0:T(8,128)(2,1)} %get-tuple-element.44.refs_2_, ...), custom_call_target="tpu_custom_call" | custom-call | tf_op jit(solution)/shard_map/reduce_layer_2/pallas_call | solution.py:353
  292.2 9.1 %copy.22 = f32[2048,1024]{0,1:T(8,128)} copy(f32[2048,1024]{1,0:T(8,128)} %get-tuple-element.26) | data formatting | bytes 16777216 | tf_op jit(solution)/shard_map/reduce_layer_2/pallas_call | solution.py:353
  301.3 5.7 fusion.13
  307.0 0.0 copy-done.13
  307.0 6.4 %copy.21 = bf16[1,2048,1024]{1,2,0:T(8,128)(2,1)} copy(bf16[1,2048,1024]{2,1,0:T(8,128)(2,1)} %param.12) | data formatting | bytes 8388608 | tf_op args[1]
  313.5 8.7 %fusion.31 = bf16[2048,1024]{0,1:T(8,128)(2,1)} fusion(bf16[2048,1024]{0,1:T(8,128)(2,1)} %get-tuple-element.48, f32[2048,1024]{0,1:T(8,128)} %copy.22, bf16[1,2048,1024]{1,2,0:T(8,128)(2,1)} %copy.21, f32[2048]{0:T(1024)S(1)} %fusion.45, f32[2048]{0:T(1024)S(1)} %add_rsqrt_fusion), kind=kLoop, calls=%fused_computation.51 | loop fusion | flops 12582912 | bytes 20987904 | tf_op jit(solution)/shard_map/add | solution.py:430
  322.2 33.8 %fusion.5 = (bf16[2048,2816]{1,0:T(8,128)(2,1)}, bf16[2048,2816]{1,0:T(8,128)(2,1)}) fusion(f32[2048,2816]{1,0:T(8,128)} %fusion.22, f32[2048,2816]{1,0:T(8,128)} %get-tuple-element.46, bf16[2048,1024]{0,1:T(8,128)(2,1)} %fusion.31, bf16[2,2816,1024]{2,1,0:T(8,128)(2,1)} %param.15), kind=kOutput, calls=%fused_computation.9 | convolution fusion | flops 11897667584 | bytes 79167488 | tf_op jit(solution)/shard_map/dot_general | solution.py:16
  356.0 18.3 %convolution_convert_fusion.2 = bf16[2816,1024]{1,0:T(8,128)(2,1)} fusion(bf16[2048,2816]{1,0:T(8,128)(2,1)} %get-tuple-element.45, bf16[2048,1024]{0,1:T(8,128)(2,1)} %fusion.31), kind=kOutput, calls=%fused_computation.47 | convolution fusion | flops 11814043648 | bytes 21495808 | tf_op jit(solution)/shard_map/dot_general | solution.py:16
  374.3 0.0 copy-done
  374.3 0.0 copy-done.11
  374.3 3.2 fusion.32.refs_0_
  377.5 78.5 %reduce_layer_1.1 = (bf16[64,5632]{1,0:T(8,128)(2,1)}, bf16[176,1024]{1,0:T(8,128)(2,1)}, f32[8,128]{1,0:T(8,128)}) custom-call(bf16[1024,2048]{1,0:T(8,128)(2,1)} %fusion.32.refs_0_, bf16[2,2,2,2,176,1024]{5,4,3,2,1,0:T(8,128)(2,1)} %bitcast.75, bf16[2048,2816]{1,0:T(8,128)(2,1)} %get-tuple-element.42.refs_2_, bf16[2048,2816]{1,0:T(8,128)(2,1)} %get-tuple-element.41.refs_3_), custom_call_target="tpu_custom_call" | custom-call | tf_op jit(solution)/shard_map/reduce_layer_1/pallas_call | solution.py:353
  455.9 0.0 copy-done.14
  456.0 1.3 add.51.sq
  457.2 127.7 %step_and_gather.1 = (bf16[2,2,2,2,2,64,2816]{6,5,4,3,2,1,0:T(8,128)(2,1)}, bf16[2,2,2,2,2,64,2816]{6,5,4,3,2,1,0:T(8,128)(2,1)}, bf16[2,2,2,2,2,176,1024]{6,5,4...) custom-call(f32[8,128]{1,0:T(8,128)} %add.51.sq, ...), custom_call_target="tpu_custom_call" | custom-call | tf_op jit(solution)/shard_map/step_and_gather/pallas_call | solution.py:148
  584.9 0.0 slice-start
  584.9 0.0 slice-start.1
  584.9 11.7 %copy.33 = bf16[2,1024,2816]{2,1,0:T(8,128)(2,1)} copy(bf16[2,1024,2816]{2,1,0:T(8,128)(2,1)} %bitcast.72) | data formatting | bytes 23068672
  596.6 0.0 copy-done.3
  596.6 5.8 copy.34
  602.4 0.7 slice-done.1
  603.1 1.3 slice-done.2
  604.4 5.4 copy.35
  609.8 0.0 copy-done.9
  609.8 1.1 copy.36
  610.9 1.1 copy.37
  612.0 0.0 copy-done.7
  612.0 1.1 copy.38
  613.1 1.1 copy.39
  614.2 1.1 copy.40
  615.4 1.1 copy.41
  (23 shorter events, 0.1 us)
Async XLA Ops:
  10.2 19.9 %copy-start.10 = (f32[2048]{0:T(1024)}, f32[2048]{0:T(1024)S(1)}, u32[]{:S(2)}) copy-start(f32[2048]{0:T(1024)S(1)} %add_rsqrt_fusion.1) | copy-start | bytes 24580
  78.3 20.3 %copy-start.12 = (f32[2048]{0:T(1024)}, f32[2048]{0:T(1024)S(1)}, u32[]{:S(2)}) copy-start(f32[2048]{0:T(1024)S(1)} %get-tuple-element.47) | copy-start | bytes 24580
  78.4 20.3 %copy-start.1 = (bf16[2048,1024]{0,1:T(8,128)(2,1)S(1)}, bf16[2048,1024]{0,1:T(8,128)(2,1)}, u32[]{:S(2)}) copy-start(bf16[2048,1024]{0,1:T(8,128)(2,1)} %get-tuple-element.48) | copy-start | bytes 12582916
  150.9 23.6 %copy-start.2 = (bf16[2048,1024]{0,1:T(8,128)(2,1)S(1)}, bf16[2048,1024]{0,1:T(8,128)(2,1)}, u32[]{:S(2)}) copy-start(bf16[2048,1024]{0,1:T(8,128)(2,1)} %get-tuple-element.48) | copy-start | bytes 12582916
  301.3 5.7 copy-start.13
  356.0 18.3 %copy-start = (bf16[1,2048,1024]{1,2,0:T(8,128)(2,1)S(1)}, bf16[1,2048,1024]{1,2,0:T(8,128)(2,1)}, u32[]{:S(2)}) copy-start(bf16[1,2048,1024]{1,2,0:T(8,128)(2,1)} %copy.20) | copy-start | bytes 12582916
  356.0 18.3 %copy-start.11 = (f32[2048]{0:T(1024)S(1)}, f32[2048]{0:T(1024)}, u32[]{:S(2)}) copy-start(f32[2048]{0:T(1024)} %copy-done.10) | copy-start | bytes 24580
  377.5 78.5 %copy-start.14 = (f32[8,128]{1,0:T(8,128)S(1)}, f32[8,128]{1,0:T(8,128)}, u32[]{:S(2)}) copy-start(f32[8,128]{1,0:T(8,128)} %get-tuple-element.25) | copy-start | bytes 12292
  584.9 11.7 %copy-start.3 = (bf16[2,2,2,2,2,64,2816]{6,5,4,3,2,1,0:T(8,128)(2,1)S(1)}, bf16[2,2,2,2,2,64,2816]{6,5,4,3,2,1,0:T(8,128)(2,1)}, u32[]{:S(2)}) copy-start(bf16[2,2,2,2,2,64,2816]{6,5,4,3,2,1,0:T(8,128)(2,1)} %get-tuple-element.33) | copy-start | bytes 34603012
  584.9 17.6 %slice-start = ((s8[11534336]{0:T(1024)(128)(4,1)}), s8[4194304]{0:T(1024)(128)(4,1)S(1)}, s32[]{:S(2)}) async-start(s8[11534336]{0:T(1024)(128)(4,1)} %bitcast.68), calls=%async_computation | async-start | bytes 8388608
  584.9 18.2 %slice-start.1 = ((s8[11534336]{0:T(1024)(128)(4,1)}), s8[4194304]{0:T(1024)(128)(4,1)S(1)}, s32[]{:S(2)}) async-start(s8[11534336]{0:T(1024)(128)(4,1)} %bitcast.68), calls=%async_computation.1 | async-start | bytes 8388608
  596.6 7.8 %slice-start.2 = ((s8[11534336]{0:T(1024)(128)(4,1)}), s8[3145728]{0:T(1024)(128)(4,1)S(1)}, s32[]{:S(2)}) async-start(s8[11534336]{0:T(1024)(128)(4,1)} %bitcast.68), calls=%async_computation.2 | async-start | bytes 6291456
  604.4 5.4 copy-start.9
  604.4 6.5 %copy-start.8 = (f32[2,64,2816]{2,1,0:T(8,128)S(1)}, f32[2,64,2816]{2,1,0:T(8,128)}, u32[]{:S(2)}) copy-start(f32[2,64,2816]{2,1,0:T(8,128)} %get-tuple-element.64) | copy-start | bytes 4325380
  604.4 7.6 %copy-start.7 = (f32[2,176,1024]{2,1,0:T(8,128)S(1)}, f32[2,176,1024]{2,1,0:T(8,128)}, u32[]{:S(2)}) copy-start(f32[2,176,1024]{2,1,0:T(8,128)} %get-tuple-element.65) | copy-start | bytes 4325380
  609.8 3.3 copy-start.6
  609.8 4.4 copy-start.5
  609.8 5.5 copy-start.4

commit v4 on v3

--- a/solution.py
+++ b/solution.py
@@ -181,16 +181,18 @@
     return sum(t[:, j : j + 128] for j in range(0, t.shape[-1], 128))
 
 
-def reduce_kernel(per, with_da, *refs):
-    a_t, down, dgate, dup, *refs = refs
+def reduce_kernel(per, l, with_da, *refs):
+    a_t, d, down, gate, up, w_down, *refs = refs
     if with_da:
-        w_gate, w_up, *refs = refs
+        w_gate, w_up, h, *refs = refs
     gu, dn, sq, *refs = refs
     if with_da:
-        da, *refs = refs
+        new_d, *refs = refs
     tile, got, kept1, kept2, kept3, out1, out2, out3, in1, in2, in3 = refs[:11]
     d_own, d_got, d_kept1, d_kept2, d_kept3, d_out1, d_out2, d_out3, d_in1, d_in2, d_in3 = refs[11:22]
-    stream, w_stream, s_sem, w_sem, send, recv, d_send, d_recv, own_sem = refs[22:]
+    gates, ups, d_gu, wd, p_sem, w_sem, send, recv, d_send, d_recv, own_sem, *refs = refs[22:]
+    if with_da:
+        da, wgu, h_part, h_sem = refs
     kept, outs, ins = (kept1, kept2, kept3), (out1, out2, out3), (in1, in2, in3)
     d_kept, d_outs, d_ins = (d_kept1, d_kept2, d_kept3), (d_out1, d_out2, d_out3), (d_in1, d_in2, d_in3)
     n_units = 2 * per
@@ -198,14 +200,16 @@
     at = [(me // s) % 2 for s in LINKS]
     core = me % 2
     everything = slice(None)
+    part = gates.shape[1]
+    parts = d.shape[0] // part
 
     def remote(src, dst, s, r, stride):
         return pltpu.make_async_remote_copy(src, dst, s, r, device_id={"dp": flipped(me, stride)}, device_id_type=MESH)
 
     def hop(u, k, stage):
         if stage == 0:
-            return remote(tile.at[u % 3, :, :, :, 1 - core], got.at[u], send.at[0, u], recv.at[0, u], 1)
-        return remote(outs[stage - 1].at[u], ins[stage - 1].at[u], send.at[stage, u], recv.at[stage, u], LINKS[(k + stage - 1) % 3])
+            return remote(tile.at[u % 3, :, :, :, 1 - core], got.at[u % 4], send.at[0, u], recv.at[0, u], 1)
+        return remote(outs[stage - 1].at[u], ins[stage - 1].at[u % 6], send.at[stage, u], recv.at[stage, u], LINKS[(k + stage - 1) % 3])
 
     def down_hop(k, stage):
         cols = pl.ds(*widths(dn.shape[1], 0)[k])
@@ -229,14 +233,14 @@
 
         def total(where):
             if stage == 1:
-                mine, other = tile[(u % 3, *where, core)], got[(u, *where)]
+                mine, other = tile[(u % 3, *where, core)], got[(u % 4, *where)]
             else:
-                mine, other = kept[stage - 2][(u % 4, *where)], ins[stage - 2][(u, *where)]
+                mine, other = kept[stage - 2][(u % 4, *where)], ins[stage - 2][(u % 6, *where)]
             return mine.astype(jnp.float32) + other.astype(jnp.float32)
 
         if stage == 4:
             g = total(()).astype(jnp.bfloat16)
-            gu[:, pl.ds(pl.multiple_of(u * UNIT, UNIT), UNIT)] = g
+            gu[:, pl.ds(pl.multiple_of((u % 2) * per * UNIT + (u // 2) * UNIT, UNIT), UNIT)] = g
             sq[...] += fold(g.astype(jnp.float32))
             return
         away, here = halves(k, stage)
@@ -264,23 +268,88 @@
         down_hop(k, stage).start()
         d_kept[stage - 1][(*rest, cols)] = total(here)
 
-    def loads(u, arrays):
-        col = pl.ds(pl.multiple_of((u % per) * UNIT, UNIT), UNIT)
-        slot = u % 2
-        pairs = [(arrays[0], stream, s_sem)] + ([(arrays[1], w_stream, w_sem)] if with_da else [])
-        return [pltpu.make_async_copy(src.at[:, col], dst.at[slot], sem.at[slot]) for src, dst, sem in pairs]
-
-    def load(u):
-        for which in range(2):
-
-            @pl.when(u // per == which)
+    def chunk(j):
+        return pl.ds(pl.multiple_of(j * UNIT, UNIT), UNIT)
+
+    def part_loads(j, p):
+        rows = pl.ds(pl.multiple_of(p * part, part), part)
+        pairs = ((gate, gates), (up, ups))
+        return [pltpu.make_async_copy(s.at[rows, chunk(j)], t.at[p], p_sem.at[i, p]) for i, (s, t) in enumerate(pairs)]
+
+    def weight_loads(j):
+        slot = j % 2
+        copies = [pltpu.make_async_copy(w_down.at[l, chunk(j)], wd.at[slot], w_sem.at[0, slot])]
+        if with_da:
+            for i, w in enumerate((w_gate, w_up)):
+                copies.append(pltpu.make_async_copy(w.at[l, :, chunk(j)], wgu.at[slot, i], w_sem.at[1 + i, slot]))
+        return copies
+
+    def start(copies):
+        for copy in copies:
+            copy.start()
+
+    def back_through(j):
+        for copy in weight_loads(j):
+            copy.wait()
+
+        @pl.when(j + 1 < per)
+        def _():
+            start(weight_loads(j + 1))
+
+        slot = j % 2
+
+        def one(p, _):
+            for copy in part_loads(j, p):
+                copy.wait()
+            rows = pl.ds(pl.multiple_of(p * part, part), part)
+            dz = lax.dot_general(d[rows], wd[slot], (((1,), (1,)), ((), ())), preferred_element_type=jnp.float32)
+            dz = dz.astype(jnp.bfloat16).astype(jnp.float32)
+            g, u = gates[p], ups[p]
+            sig = jax.nn.sigmoid(g)
+            d_u = (dz * (g * sig)).astype(jnp.bfloat16)
+            d_g = (dz * u * (sig * (1 + g * (1 - sig)))).astype(jnp.bfloat16)
+            d_gu[0, rows] = d_g
+            d_gu[1, rows] = d_u
+            if with_da:
+                da[rows] += lax.dot_general(
+                    d_g, wgu[slot, 0], (((1,), (1,)), ((), ())), preferred_element_type=jnp.float32
+                ) + lax.dot_general(d_u, wgu[slot, 1], (((1,), (1,)), ((), ())), preferred_element_type=jnp.float32)
+
+            @pl.when(j + 1 < per)
             def _():
-                for copy in loads(u, ((dgate, dup)[which], (w_gate, w_up)[which] if with_da else None)):
-                    copy.start()
+                start(part_loads(j + 1, p))
+
+        lax.fori_loop(0, parts, one, None)
+
+    def h_load(p):
+        rows = pl.ds(pl.multiple_of(p * part, part), part)
+        return pltpu.make_async_copy(h.at[rows], h_part.at[p % 2], h_sem.at[0, p % 2])
+
+    def d_store(p):
+        rows = pl.ds(pl.multiple_of(p * part, part), part)
+        return pltpu.make_async_copy(h_part.at[p % 2], new_d.at[rows], h_sem.at[1, p % 2])
+
+    def norm_back(p):
+        h_load(p).wait()
+        rows = pl.ds(pl.multiple_of(p * part, part), part)
+        wide = h_part[p % 2].astype(jnp.float32)
+        scale = lax.rsqrt(jnp.mean(wide * wide, -1, keepdims=True) + 1e-6)
+        grad = da[rows]
+        back = grad * scale - wide * (scale * scale * scale * jnp.mean(grad * wide, -1, keepdims=True))
+        total = d[rows].astype(jnp.float32) + back.astype(jnp.bfloat16).astype(jnp.float32)
+        h_part[p % 2] = total.astype(jnp.bfloat16)
+        d_store(p).start()
+
+        @pl.when(p + 2 < parts)
+        def _():
+            d_store(p).wait()
+            h_load(p + 2).start()
 
     own = pltpu.make_async_copy(down.at[:, :, :, core], d_own, own_sem)
     own.start()
-    load(0)
+    start(weight_loads(0))
+    for p in range(parts):
+        start(part_loads(0, p))
     barrier = pltpu.get_barrier_semaphore()
     for stride in (1, *LINKS):
         pl.semaphore_signal(barrier, inc=1, device_id={"dp": flipped(me, stride)}, device_id_type=MESH)
@@ -293,10 +362,6 @@
     own.wait()
 
     def step(t, _):
-        @pl.when(t + 1 < n_units)
-        def _():
-            load(t + 1)
-
         for stage, lag in reversed(list(enumerate(LAGS, 1))):
             u = t - lag
             for k in range(3):
@@ -314,21 +379,24 @@
 
         @pl.when(t < n_units)
         def _():
-            for copy in loads(t, (dgate, w_gate if with_da else None)):
-                copy.wait()
-            slot = t % 2
-            g = jnp.dot(a_t[...], stream[slot], preferred_element_type=jnp.float32).astype(jnp.bfloat16)
+            @pl.when(t % 2 == 0)
+            def _():
+                back_through(t // 2)
+
+            g = jnp.dot(a_t[...], d_gu[t % 2], preferred_element_type=jnp.float32).astype(jnp.bfloat16)
             tile[t % 3] = g.reshape(tile.shape[1:])
             hop(t, 0, 0).start()
-            if with_da:
-
-                def rows(j, _):
-                    part = pl.ds(pl.multiple_of(j * 512, 512), 512)
-                    da[part] += lax.dot_general(
-                        stream[slot, part], w_stream[slot], (((1,), (1,)), ((), ())), preferred_element_type=jnp.float32
-                    )
-
-                lax.fori_loop(0, da.shape[0] // 512, rows, None)
+
+        if with_da:
+
+            @pl.when(t == n_units - 1)
+            def _():
+                for p in range(2):
+                    h_load(p).start()
+
+            @pl.when((t >= n_units) & (t < n_units + parts))
+            def _():
+                norm_back(t - n_units)
 
     lax.fori_loop(0, n_units + LAGS[-1], step, None)
 
@@ -340,56 +408,61 @@
     for k in range(3):
         for stage in range(4):
             down_hop(k, stage).wait_send()
-
-
-def reduce_layer(a, down, dgate, dup, weights, collective_id):
-    tokens, d = a.shape
-    ff = dgate.shape[1]
-    per, rows, d_rows, with_da = ff // UNIT, d // 16, ff // 16, weights is not None
-    n_units = 2 * per
+    if with_da:
+        for p in (parts - 2, parts - 1):
+            d_store(p).wait()
+
+
+def reduce_layer(a, d, down, gate, up, w_down, l, h, weights, collective_id):
+    tokens, width = a.shape
+    ff = gate.shape[1]
+    per, rows, d_rows, with_da = ff // UNIT, width // 16, ff // 16, weights is not None
+    n_units, part = 2 * per, tokens // 4
     vmem, hbm = pl.BlockSpec(memory_space=pltpu.VMEM), pl.BlockSpec(memory_space=pl.ANY)
     dma, b16, f32 = pltpu.SemaphoreType.DMA, jnp.bfloat16, jnp.float32
-    whole = [jax.ShapeDtypeStruct((tokens, d), f32)] if with_da else []
     return pl.pallas_call(
-        functools.partial(reduce_kernel, per, with_da),
+        functools.partial(reduce_kernel, per, l, with_da),
         out_shape=[
             jax.ShapeDtypeStruct((rows, 2 * ff), b16),
-            jax.ShapeDtypeStruct((d_rows, d), b16),
+            jax.ShapeDtypeStruct((d_rows, width), b16),
             jax.ShapeDtypeStruct((8, 128), f32),
         ]
-        + whole,
-        in_specs=[vmem] + [hbm] * (5 if with_da else 3),
-        out_specs=[vmem] * (3 + len(whole)),
+        + [jax.ShapeDtypeStruct((tokens, width), b16)] * with_da,
+        in_specs=[vmem] * 2 + [hbm] * (7 if with_da else 4),
+        out_specs=[vmem] * 3 + [hbm] * with_da,
         scratch_shapes=[
             pltpu.VMEM((3, 2, 2, 2, 2, rows, UNIT), b16),
-            pltpu.VMEM((n_units, 2, 2, 2, rows, UNIT), b16),
+            pltpu.VMEM((4, 2, 2, 2, rows, UNIT), b16),
             pltpu.VMEM((4, 2, 2, rows, UNIT), f32),
             pltpu.VMEM((4, 2, rows, UNIT), f32),
             pltpu.VMEM((4, rows, UNIT), f32),
         ]
-        + [
-            pltpu.VMEM((n_units, 2, 2, rows, UNIT), b16),
-            pltpu.VMEM((n_units, 2, rows, UNIT), b16),
-            pltpu.VMEM((n_units, rows, UNIT), b16),
-        ]
-        * 2
-        + [pltpu.VMEM((2, 2, 2, d_rows, d), b16)] * 2
-        + [pltpu.VMEM((2, 2, d_rows, d), f32), pltpu.VMEM((2, d_rows, d), f32), pltpu.VMEM((d_rows, d), f32)]
-        + [pltpu.VMEM((2, 2, d_rows, d), b16), pltpu.VMEM((2, d_rows, d), b16), pltpu.VMEM((d_rows, d), b16)] * 2
+        + [pltpu.VMEM((slots, *lead, rows, UNIT), b16) for slots in (n_units, 6) for lead in ((2, 2), (2,), ())]
+        + [pltpu.VMEM((2, 2, 2, d_rows, width), b16)] * 2
+        + [pltpu.VMEM((2, 2, d_rows, width), f32), pltpu.VMEM((2, d_rows, width), f32), pltpu.VMEM((d_rows, width), f32)]
+        + [pltpu.VMEM((2, 2, d_rows, width), b16), pltpu.VMEM((2, d_rows, width), b16), pltpu.VMEM((d_rows, width), b16)] * 2
+        + [pltpu.VMEM((4, part, UNIT), f32)] * 2
         + [
             pltpu.VMEM((2, tokens, UNIT), b16),
-            pltpu.VMEM((2, d, UNIT), b16),
-            dma((2,)),
-            dma((2,)),
+            pltpu.VMEM((2, UNIT, width), b16),
+            dma((2, 4)),
+            dma((3, 2)),
             dma((4, n_units)),
             dma((4, n_units)),
             dma((4, 3)),
             dma((4, 3)),
             dma(()),
-        ],
-        compiler_params=pltpu.CompilerParams(collective_id=collective_id, has_side_effects=True, vmem_limit_bytes=62 * 2**20),
+        ]
+        + [
+            pltpu.VMEM((tokens, width), f32),
+            pltpu.VMEM((2, 2, width, UNIT), b16),
+            pltpu.VMEM((2, part, width), b16),
+            dma((2, 2)),
+        ]
+        * with_da,
+        compiler_params=pltpu.CompilerParams(collective_id=collective_id, has_side_effects=True, vmem_limit_bytes=63 * 2**20),
         name=f"reduce_layer_{collective_id}",
-    )(a.T, down.reshape(2, 2, 2, 2, d_rows, d), dgate, dup, *(weights or ()))
+    )(a.T, d, down.reshape(2, 2, 2, 2, d_rows, width), gate, up, w_down, *((*weights, h) if with_da else ()))
 
 
 def solution(mesh):
@@ -415,19 +488,12 @@
         for l in reversed(range(layers)):
             h, scale, a, gate, up, z = saved[l]
             down = dot(z, d, ((0,), (0,))).astype(jnp.bfloat16)
-            dz = dot(d, w_down[l], ((1,), (1,))).astype(jnp.bfloat16).astype(jnp.float32)
-            sig = jax.nn.sigmoid(gate)
-            silu = gate * sig
-            dup = (dz * silu).astype(jnp.bfloat16)
-            dgate = (dz * up * (sig * (1 + gate * (1 - sig)))).astype(jnp.bfloat16)
-            gu, dn, sq, *da = reduce_layer(a, down, dgate, dup, (w_gate[l], w_up[l]) if l else None, l + 1)
+            weights = (w_gate, w_up) if l else None
+            gu, dn, sq, *new_d = reduce_layer(a, d, down, gate, up, w_down, l, h, weights, l + 1)
             summed[l] = (gu, dn)
             squares = squares + sq
             if l:
-                da = da[0]
-                wide = h.astype(jnp.float32)
-                back = da * scale - wide * (scale**3 * jnp.mean(da * wide, -1, keepdims=True))
-                d = d + back.astype(jnp.bfloat16)
+                d = new_d[0]
 
         gu, dn = zip(*summed, strict=True)
         count = sum(t.size for t in m) * n

time: 624 us -> 561 us (0.90)
  matrix products: 216 us -> 144 us
  Pallas kernels: 311 us -> 349 us
  local copies, waits for them, and re-layouts: 62.9 us -> 44.5 us
  other arithmetic: 25.1 us -> 15.6 us
    dot_general x9 -> x7, matrix products: 216 us -> 144 us  [dot(): lax.dot_general(a, b, (dims, ((), ())), preferred_element_type=jnp.float32)]
    pallas_call x2, Pallas kernels: 184 us -> 221 us  [reduce_layer(): pl.pallas_call(functools.partial(reduce_kernel, per, l, with_da), out_sha...]
    squeeze x1 -> x0, local copies, waits for them, and re-layouts: 9.27 us -> none  [step(): up = dot(a, w_up[l], ((1,), (0,)))]
    pallas_call x1 -> x0, local copies, waits for them, and re-layouts: 9.13 us -> none  [reduce_layer(): pl.pallas_call(functools.partial(reduce_kernel, per, with_da), out_shape=...]
    add x1 -> x0, other arithmetic: 8.69 us -> none  [step(): d = d + back.astype(jnp.bfloat16)]
    add x0 -> x1, local copies, waits for them, and re-layouts: none -> 6.53 us  [step(): h = h + dot(z, w_down[l], ((1,), (0,))).astype(jnp.bfloat16)]
    unnamed x47 -> x42, local copies, waits for them, and re-layouts: 44.5 us -> 38 us
where the time goes in v4:
time: 561 us; the launch traced here: 555 us
  Pallas kernels  349 us (62%)
  matrix products  144 us (26%)
  local copies, waits for them, and re-layouts  44.5 us (8%)
  other arithmetic  15.6 us (3%)
    pallas_call x2, Pallas kernels, reduce_layer(): pl.pallas_call(functools.partial(reduce_kernel, per, l, with_da), out_sha...  221 us
    dot_general x7, matrix products, dot(): lax.dot_general(a, b, (dims, ((), ())), preferred_element_type=jnp.float32)  144 us
    pallas_call x1, Pallas kernels, step_and_gather(): pl.pallas_call(functools.partial(gather_kernel, shapes, count), out_shape...  128 us
    unnamed x42, local copies, waits for them, and re-layouts  38 us

profile of v4, /device:TPU:0, one launch (start us, length us, event | category | flops | bytes accessed | tf_op | source)
XLA Modules:
  0.0 554.8 jit_solution(13343727735710920535)
XLA Ops:
  0.6 6.4 %copy.20 = bf16[1,2048,1024]{1,2,0:T(8,128)(2,1)} copy(bf16[1,2048,1024]{2,1,0:T(8,128)(2,1)} %param.11) | data formatting | bytes 8388608 | tf_op args[0]
  7.1 0.0 copy-start.2
  7.1 3.2 fusion.1
  10.3 5.5 fusion.22.refs_0_
  15.8 0.0 copy-done.2
  15.8 18.2 %fusion.13.refs_3_ = f32[2048,2816]{1,0:T(8,128)} fusion(bf16[2,1024,2816]{2,1,0:T(8,128)(2,1)} %refs_6_.1, bf16[1,2048,1024]{2,1,0:T(8,128)(2,1)S(1)} %copy-done.2, f32[2048]{0:T(1024)S(1)} %add_rsqrt_fusion.1), kind=kOutput, calls=%fused_computation.20 | convolution fusion | flops 11817451520 | bytes 33038336 | tf_op jit(solution)/shard_map/dot_general | solution.py:16
  34.1 28.6 %multiply_convert_fusion.1 = (bf16[2048,2816]{1,0:T(8,128)(2,1)}, f32[2048,2816]{1,0:T(8,128)}) fusion(f32[2048,2816]{1,0:T(8,128)} %fusion.13.refs_3_, bf16[2,1024,2816]{2,1,0:T(8,128)(2,1)} %refs_7_.2, bf16[1,2048,1024]{2,1,0:T(8,128)(2,1)} %param.11, f32[2048]{0:T(1024)S(1)} %add_rsqrt_fusion.1), kind=kOutput, calls=%fused_computation.1 | convolution fusion | flops 11852054528 | bytes 67641344 | tf_op jit(solution)/shard_map/dot_general | solution.py:16
  62.7 19.8 %fusion.3 = (f32[2048]{0:T(1024)S(1)}, bf16[2048,1024]{0,1:T(8,128)(2,1)}) fusion(bf16[2048,2816]{1,0:T(8,128)(2,1)} %get-tuple-element.41, bf16[2,2816,1024]{2,1,0:T(8,128)(2,1)} %refs_5_.3, bf16[1,2048,1024]{1,2,0:T(8,128)(2,1)} %copy.20), kind=kOutput, calls=%fused_computation.9 | convolution fusion | flops 11821643776 | bytes 25698304 | tf_op jit(solution)/shard_map/dot_general | solution.py:16
  82.6 5.6 %fusion.27.refs_0_ = bf16[1024,2048]{1,0:T(8,128)(2,1)} fusion(f32[2048]{0:T(1024)S(1)} %add_rsqrt_fusion, bf16[2048,1024]{0,1:T(8,128)(2,1)} %get-tuple-element.44), kind=kLoop, calls=%fused_computation.32 | loop fusion | flops 6291456 | bytes 8396800 | tf_op jit(solution)/shard_map/transpose | solution.py:465
  88.1 0.0 slice-start
  88.1 6.5 %copy.21.refs_8_ = bf16[2048,1024]{1,0:T(8,128)(2,1)} copy(bf16[2048,1024]{0,1:T(8,128)(2,1)} %get-tuple-element.44) | data formatting | bytes 8388608 | tf_op jit(solution)/shard_map/add | solution.py:485
  94.7 0.0 slice-start.1
  94.7 0.0 slice-start.2
  94.7 20.2 %fusion.7.refs_3_ = f32[2048,2816]{1,0:T(8,128)} fusion(bf16[2,1024,2816]{2,1,0:T(8,128)(2,1)} %refs_6_.1, bf16[2048,1024]{0,1:T(8,128)(2,1)} %get-tuple-element.44, f32[2048]{0:T(1024)S(1)} %add_rsqrt_fusion), kind=kOutput, calls=%fused_computation.14 | convolution fusion | flops 11817451520 | bytes 33038336 | tf_op jit(solution)/shard_map/dot_general | solution.py:16
  114.9 0.0 slice-done
  114.9 0.0 slice-done.1
  114.9 0.0 slice-done.2
  114.9 0.0 copy-done
  114.9 15.4 %fusion.5.refs_4_ = f32[2048,2816]{1,0:T(8,128)} fusion(bf16[2,1024,2816]{2,1,0:T(8,128)(2,1)S(1)} %bitcast.53, bf16[2048,1024]{0,1:T(8,128)(2,1)S(1)} %copy-done, f32[2048]{0:T(1024)S(1)} %add_rsqrt_fusion), kind=kOutput, calls=%fused_computation.12 | convolution fusion | flops 11817451520 | bytes 33038336 | tf_op jit(solution)/shard_map/dot_general | solution.py:16
  130.3 23.8 %fusion.20 = bf16[2816,1024]{1,0:T(8,128)(2,1)} fusion(f32[2048,2816]{1,0:T(8,128)} %fusion.5.refs_4_, f32[2048,2816]{1,0:T(8,128)} %fusion.7.refs_3_, bf16[1,2048,1024]{2,1,0:T(8,128)(2,1)} %param.12), kind=kOutput, calls=%fused_computation.27 | convolution fusion | flops 11848646656 | bytes 56098816 | tf_op jit(solution)/shard_map/dot_general | solution.py:16
  154.1 132.5 %reduce_layer_2.1 = (bf16[64,5632]{1,0:T(8,128)(2,1)}, bf16[176,1024]{1,0:T(8,128)(2,1)}, f32[8,128]{1,0:T(8,128)}, bf16[2048,1024]{1,0:T(8,128)(2,1)}) custom-call(bf16[1024,2048]{1,0:T(8,128)(2,1)} %fusion.27.refs_0_, bf16[2048,1024]{1,0:T(8,128)(2,1)} %bitcast.61, bf16[2,2,2,2,176,1024]{5,4,3,2,1,0:T(8,128)(2,1)} %bitcast.59, ...), custom_call_target="tpu_custom_call" | custom-call | tf_op jit(solution)/shard_map/reduce_layer_2/pallas_call | solution.py:423
  286.7 18.1 %convolution_convert_fusion = bf16[2816,1024]{1,0:T(8,128)(2,1)} fusion(bf16[2048,2816]{1,0:T(8,128)(2,1)} %get-tuple-element.41, bf16[2048,1024]{1,0:T(8,128)(2,1)} %get-tuple-element.26.refs_1_), kind=kOutput, calls=%fused_computation.28 | convolution fusion | flops 11814043648 | bytes 21495808 | tf_op jit(solution)/shard_map/dot_general | solution.py:16
  304.8 88.6 %reduce_layer_1.1 = (bf16[64,5632]{1,0:T(8,128)(2,1)}, bf16[176,1024]{1,0:T(8,128)(2,1)}, f32[8,128]{1,0:T(8,128)}) custom-call(bf16[1024,2048]{1,0:T(8,128)(2,1)} %fusion.22.refs_0_, bf16[2048,1024]{1,0:T(8,128)(2,1)} %get-tuple-element.26.refs_1_, bf16[2,2,2,2,176,1024]{5,4,3,2,1,0:T(8,128)(2,1)} %bitcast.60, f32[2048,2816]{1,0:T(8,128)} %fusion.13.refs_3_, ...), custom_call_target="tpu_custom_call" | custom-call | tf_op jit(solution)/shard_map/reduce_layer_1/pallas_call | solution.py:423
  393.4 0.0 copy-done.9
  393.4 1.3 add.34.sq
  394.7 128.0 %step_and_gather.1 = (bf16[2,2,2,2,2,64,2816]{6,5,4,3,2,1,0:T(8,128)(2,1)}, bf16[2,2,2,2,2,64,2816]{6,5,4,3,2,1,0:T(8,128)(2,1)}, bf16[2,2,2,2,2,176,1024]{6,5,4...) custom-call(f32[8,128]{1,0:T(8,128)} %add.34.sq, ...), custom_call_target="tpu_custom_call" | custom-call | tf_op jit(solution)/shard_map/step_and_gather/pallas_call | solution.py:148
  522.7 0.0 copy-start.1
  522.7 0.0 slice-start.3
  522.7 0.0 slice-start.4
  522.7 11.7 %copy.31 = bf16[2,1024,2816]{2,1,0:T(8,128)(2,1)} copy(bf16[2,1024,2816]{2,1,0:T(8,128)(2,1)} %bitcast.58) | data formatting | bytes 23068672
  534.4 0.0 copy-done.1
  534.4 5.8 %copy.32 = bf16[2,1024,2816]{2,1,0:T(8,128)(2,1)} copy(bf16[2,1024,2816]{2,1,0:T(8,128)(2,1)S(1)} %bitcast.57) | data formatting | bytes 23068672
  540.3 0.0 slice-done.3
  540.3 0.7 slice-done.4
  540.9 1.3 slice-done.5
  542.3 5.4 copy.33
  547.6 0.0 copy-done.8
  547.6 1.1 copy.34
  548.7 0.0 copy-done.7
  548.7 1.1 copy.35
  549.8 0.0 copy-done.6
  549.8 1.1 copy.36
  550.9 0.0 copy-done.5
  551.0 1.1 copy.37
  552.1 0.0 copy-done.4
  552.1 1.1 copy.38
  553.2 0.0 copy-done.3
  553.2 1.1 copy.39
  (13 shorter events, 0.0 us)
Async XLA Ops:
  7.1 8.7 %copy-start.2 = (bf16[1,2048,1024]{2,1,0:T(8,128)(2,1)S(1)}, bf16[1,2048,1024]{2,1,0:T(8,128)(2,1)}, u32[]{:S(2)}) copy-start(bf16[1,2048,1024]{2,1,0:T(8,128)(2,1)} %param.11) | copy-start | bytes 12582916
  88.1 26.8 %slice-start = ((s8[11534336]{0:T(1024)(128)(4,1)}), s8[3145728]{0:T(1024)(128)(4,1)S(1)}, s32[]{:S(2)}) async-start(s8[11534336]{0:T(1024)(128)(4,1)} %bitcast.52), calls=%async_computation | async-start | bytes 6291456
  94.7 20.2 %slice-start.1 = ((s8[11534336]{0:T(1024)(128)(4,1)}), s8[4194304]{0:T(1024)(128)(4,1)S(1)}, s32[]{:S(2)}) async-start(s8[11534336]{0:T(1024)(128)(4,1)} %bitcast.52), calls=%async_computation.1 | async-start | bytes 8388608
  94.7 20.2 %slice-start.2 = ((s8[11534336]{0:T(1024)(128)(4,1)}), s8[4194304]{0:T(1024)(128)(4,1)S(1)}, s32[]{:S(2)}) async-start(s8[11534336]{0:T(1024)(128)(4,1)} %bitcast.52), calls=%async_computation.2 | async-start | bytes 8388608
  94.7 20.2 %copy-start = (bf16[2048,1024]{0,1:T(8,128)(2,1)S(1)}, bf16[2048,1024]{0,1:T(8,128)(2,1)}, u32[]{:S(2)}) copy-start(bf16[2048,1024]{0,1:T(8,128)(2,1)} %get-tuple-element.44) | copy-start | bytes 12582916
  304.8 88.6 %copy-start.9 = (f32[8,128]{1,0:T(8,128)S(1)}, f32[8,128]{1,0:T(8,128)}, u32[]{:S(2)}) copy-start(f32[8,128]{1,0:T(8,128)} %get-tuple-element.25) | copy-start | bytes 12292
  522.7 11.7 %copy-start.1 = (bf16[2,2,2,2,2,64,2816]{6,5,4,3,2,1,0:T(8,128)(2,1)S(1)}, bf16[2,2,2,2,2,64,2816]{6,5,4,3,2,1,0:T(8,128)(2,1)}, u32[]{:S(2)}) copy-start(bf16[2,2,2,2,2,64,2816]{6,5,4,3,2,1,0:T(8,128)(2,1)} %get-tuple-element.33) | copy-start | bytes 34603012
  522.7 17.6 %slice-start.3 = ((s8[11534336]{0:T(1024)(128)(4,1)}), s8[4194304]{0:T(1024)(128)(4,1)S(1)}, s32[]{:S(2)}) async-start(s8[11534336]{0:T(1024)(128)(4,1)} %bitcast.54), calls=%async_computation.3 | async-start | bytes 8388608
  522.7 18.2 %slice-start.4 = ((s8[11534336]{0:T(1024)(128)(4,1)}), s8[4194304]{0:T(1024)(128)(4,1)S(1)}, s32[]{:S(2)}) async-start(s8[11534336]{0:T(1024)(128)(4,1)} %bitcast.54), calls=%async_computation.4 | async-start | bytes 8388608
  534.4 7.8 %slice-start.5 = ((s8[11534336]{0:T(1024)(128)(4,1)}), s8[3145728]{0:T(1024)(128)(4,1)S(1)}, s32[]{:S(2)}) async-start(s8[11534336]{0:T(1024)(128)(4,1)} %bitcast.54), calls=%async_computation.5 | async-start | bytes 6291456
  542.2 5.4 copy-start.8
  542.2 6.5 %copy-start.7 = (f32[2,64,2816]{2,1,0:T(8,128)S(1)}, f32[2,64,2816]{2,1,0:T(8,128)}, u32[]{:S(2)}) copy-start(f32[2,64,2816]{2,1,0:T(8,128)} %get-tuple-element.58) | copy-start | bytes 4325380
  542.3 7.6 %copy-start.6 = (f32[2,176,1024]{2,1,0:T(8,128)S(1)}, f32[2,176,1024]{2,1,0:T(8,128)}, u32[]{:S(2)}) copy-start(f32[2,176,1024]{2,1,0:T(8,128)} %get-tuple-element.59) | copy-start | bytes 4325380
  547.6 3.3 copy-start.5
  547.6 4.4 copy-start.4
  547.6 5.5 copy-start.3

commit v5 on v4

--- a/solution.py
+++ b/solution.py
@@ -176,6 +176,72 @@
 DOWN_STEPS = (3, 9, 14, 18)
 
 
+def forward_kernel(last, h, w_gate, w_up, *refs):
+    if last:
+        gate, up, z_t, a_t, a = refs
+    else:
+        w_down, gate, up, z_t, a_t, new_h, a, total = refs
+    j, part = pl.program_id(0), h.shape[0] // 4
+
+    def over_parts(body):
+        lax.fori_loop(0, 4, lambda p, _: body(pl.ds(pl.multiple_of(p * part, part), part)), None)
+
+    @pl.when(j == 0)
+    def _():
+        def norm(rows):
+            wide = h[rows].astype(jnp.float32)
+            scale = lax.rsqrt(jnp.mean(wide * wide, -1, keepdims=True) + 1e-6)
+            a[rows] = (wide * scale).astype(jnp.bfloat16)
+            a_t[:, rows] = a[rows].T
+            if not last:
+                total[rows] = jnp.zeros((part, total.shape[1]), jnp.float32)
+
+        over_parts(norm)
+
+    def hidden(rows):
+        g = jnp.dot(a[rows], w_gate[...], preferred_element_type=jnp.float32)
+        u = jnp.dot(a[rows], w_up[...], preferred_element_type=jnp.float32)
+        gate[rows] = g
+        up[rows] = u
+        z = (jax.nn.silu(g) * u).astype(jnp.bfloat16)
+        z_t[:, rows] = z.T
+        if not last:
+            total[rows] += jnp.dot(z, w_down[...], preferred_element_type=jnp.float32)
+
+    over_parts(hidden)
+    if not last:
+
+        @pl.when(j == pl.num_programs(0) - 1)
+        def _():
+            def leave(rows):
+                new_h[rows] = (h[rows].astype(jnp.float32) + total[rows].astype(jnp.bfloat16).astype(jnp.float32)).astype(jnp.bfloat16)
+
+            over_parts(leave)
+
+
+def forward_layer(h, w_gate, w_up, w_down, l, last):
+    tokens, d = h.shape
+    ff = w_gate.shape[2]
+    b16, f32 = jnp.bfloat16, jnp.float32
+    whole = lambda shape: pl.BlockSpec(shape, lambda j: (0, 0))
+    column = pl.BlockSpec((None, d, UNIT), lambda j: (l, 0, j))
+    hidden = pl.BlockSpec((tokens, UNIT), lambda j: (0, j))
+    return pl.pallas_call(
+        functools.partial(forward_kernel, last),
+        grid=(ff // UNIT,),
+        out_shape=[jax.ShapeDtypeStruct((tokens, ff), f32)] * 2
+        + [jax.ShapeDtypeStruct((ff, tokens), b16), jax.ShapeDtypeStruct((d, tokens), b16)]
+        + [jax.ShapeDtypeStruct((tokens, d), b16)] * (not last),
+        in_specs=[whole((tokens, d)), column, column]
+        + [pl.BlockSpec((None, UNIT, d), lambda j: (l, j, 0))] * (not last),
+        out_specs=[hidden, hidden, pl.BlockSpec((UNIT, tokens), lambda j: (j, 0)), whole((d, tokens))]
+        + [whole((tokens, d))] * (not last),
+        scratch_shapes=[pltpu.VMEM((tokens, d), b16)] + [pltpu.VMEM((tokens, d), f32)] * (not last),
+        compiler_params=pltpu.CompilerParams(dimension_semantics=("arbitrary",), vmem_limit_bytes=60 * 2**20),
+        name=f"forward_layer_{l}",
+    )(h, w_gate, w_up, *(() if last else (w_down,)))
+
+
 def fold(t):
     t = jnp.sum(jnp.square(t).reshape(-1, 8, t.shape[-1]), axis=0)
     return sum(t[:, j : j + 128] for j in range(0, t.shape[-1], 128))
@@ -413,8 +479,8 @@
             d_store(p).wait()
 
 
-def reduce_layer(a, d, down, gate, up, w_down, l, h, weights, collective_id):
-    tokens, width = a.shape
+def reduce_layer(a_t, d, down, gate, up, w_down, l, h, weights, collective_id):
+    width, tokens = a_t.shape
     ff = gate.shape[1]
     per, rows, d_rows, with_da = ff // UNIT, width // 16, ff // 16, weights is not None
     n_units, part = 2 * per, tokens // 4
@@ -462,7 +528,7 @@
         * with_da,
         compiler_params=pltpu.CompilerParams(collective_id=collective_id, has_side_effects=True, vmem_limit_bytes=63 * 2**20),
         name=f"reduce_layer_{collective_id}",
-    )(a.T, d, down.reshape(2, 2, 2, 2, d_rows, width), gate, up, w_down, *((*weights, h) if with_da else ()))
+    )(a_t, d, down.reshape(2, 2, 2, 2, d_rows, width), gate, up, w_down, *((*weights, h) if with_da else ()))
 
 
 def solution(mesh):
@@ -474,22 +540,17 @@
         h = x[0]
         saved = []
         for l in range(layers):
-            wide = h.astype(jnp.float32)
-            scale = lax.rsqrt(jnp.mean(wide**2, -1, keepdims=True) + 1e-6)
-            a = (wide * scale).astype(jnp.bfloat16)
-            gate = dot(a, w_gate[l], ((1,), (0,)))
-            up = dot(a, w_up[l], ((1,), (0,)))
-            z = (jax.nn.silu(gate) * up).astype(jnp.bfloat16)
-            saved.append((h, scale, a, gate, up, z))
-            if l + 1 < layers:
-                h = h + dot(z, w_down[l], ((1,), (0,))).astype(jnp.bfloat16)
+            last = l + 1 == layers
+            gate, up, z_t, a_t, *new_h = forward_layer(h, w_gate, w_up, w_down, l, last)
+            saved.append((h, a_t, gate, up, z_t))
+            h = h if last else new_h[0]
         d = dy[0]
         summed, squares = [None] * layers, 0.0
         for l in reversed(range(layers)):
-            h, scale, a, gate, up, z = saved[l]
-            down = dot(z, d, ((0,), (0,))).astype(jnp.bfloat16)
+            h, a_t, gate, up, z_t = saved[l]
+            down = dot(z_t, d, ((1,), (0,))).astype(jnp.bfloat16)
             weights = (w_gate, w_up) if l else None
-            gu, dn, sq, *new_d = reduce_layer(a, d, down, gate, up, w_down, l, h, weights, l + 1)
+            gu, dn, sq, *new_d = reduce_layer(a_t, d, down, gate, up, w_down, l, h, weights, l + 1)
             summed[l] = (gu, dn)
             squares = squares + sq
             if l:

time: 561 us -> 517 us (0.922); the launches traced: 555 us -> 516 us
  matrix products: 144 us -> 35.5 us
  Pallas kernels: 349 us -> 448 us
  other arithmetic: 15.6 us -> 1.27 us
  local copies, waits for them, and re-layouts: 44.5 us -> 31 us
    dot_general x7 -> x2, matrix products: 144 us -> 35.5 us  [dot(): lax.dot_general(a, b, (dims, ((), ())), preferred_element_type=jnp.float32)]
    pallas_call x0 -> x2, Pallas kernels: none -> 99.1 us  [forward_layer(): pl.pallas_call(functools.partial(forward_kernel, last), grid=(ff // UNIT,...]
    transpose x2 -> x0, other arithmetic: 11.1 us -> none  [reduce_layer(): return pl.pallas_call(functools.partial(reduce_kernel, per, l, with_da),...]
    unnamed x42 -> x31, local copies, waits for them, and re-layouts: 38 us -> 31 us
    add x1 -> x0, local copies, waits for them, and re-layouts: 6.53 us -> none  [step(): h = h + dot(z, w_down[l], ((1,), (0,))).astype(jnp.bfloat16)]
where the time goes in v5:
time: 517 us; the launch traced here: 516 us
  Pallas kernels  448 us (87%)
  matrix products  35.5 us (7%)
  local copies, waits for them, and re-layouts  31 us (6%)
    pallas_call x2, Pallas kernels, reduce_layer(): pl.pallas_call(functools.partial(reduce_kernel, per, l, with_da), out_sha...  221 us
    pallas_call x1, Pallas kernels, step_and_gather(): pl.pallas_call(functools.partial(gather_kernel, shapes, count), out_shape...  128 us
    pallas_call x2, Pallas kernels, forward_layer(): pl.pallas_call(functools.partial(forward_kernel, last), grid=(ff // UNIT,...  99.1 us
    dot_general x2, matrix products, dot(): lax.dot_general(a, b, (dims, ((), ())), preferred_element_type=jnp.float32)  35.5 us
    unnamed x31, local copies, waits for them, and re-layouts  31 us

profile of v5, /device:TPU:0, one launch (start us, length us, event | category | flops | bytes accessed | tf_op | source)
XLA Modules:
  0.0 516.5 jit_solution(6604251126042621983)
XLA Ops:
  0.6 56.1 %forward_layer_0.1 = (f32[2048,2816]{1,0:T(8,128)}, f32[2048,2816]{1,0:T(8,128)}, bf16[2816,2048]{1,0:T(8,128)(2,1)}, bf16[1024,2048]{1,0:T(8,128)(2,1)}, bf16[2048,1024]{1,0:T(8,128)(2,1)}) custom-call(bf16[2048,1024]{1,0:T(8,128)(2,1)} %bitcast.25, bf16[2,1024,2816]{2,1,0:T(8,128)(2,1)} %refs_6_.1, bf16[2,1024,2816]{2,1,0:T(8,128)(2,1)} %refs_7_.2, ...), custom_call_target="tpu_custom_call" | custom-call | tf_op jit(solution)/shard_map/forward_layer_0/pallas_call | solution.py:229
  56.8 43.0 %forward_layer_1.1 = (f32[2048,2816]{1,0:T(8,128)}, f32[2048,2816]{1,0:T(8,128)}, bf16[2816,2048]{1,0:T(8,128)(2,1)}, bf16[1024,2048]{1,0:T(8,128)(2,1)}) custom-call(bf16[2048,1024]{1,0:T(8,128)(2,1)} %get-tuple-element.34.h.refs_8_, bf16[2,1024,2816]{2,1,0:T(8,128)(2,1)} %refs_6_.1, bf16[2,1024,2816]{2,1,0:T(8,128)(2,1)} %refs_7_.2), custom_call_target="tpu_custom_call" | custom-call | tf_op jit(solution)/shard_map/forward_layer_1/pallas_call | solution.py:229
  99.8 17.8 %convolution_convert_fusion.1 = bf16[2816,1024]{1,0:T(8,128)(2,1)} fusion(bf16[2816,2048]{1,0:T(8,128)(2,1)} %get-tuple-element.36, bf16[1,2048,1024]{2,1,0:T(8,128)(2,1)} %param.12), kind=kOutput, calls=%fused_computation.1 | convolution fusion | flops 11814043648 | bytes 21495808 | tf_op jit(solution)/shard_map/dot_general | solution.py:16
  117.6 132.5 %reduce_layer_2.1 = (bf16[64,5632]{1,0:T(8,128)(2,1)}, bf16[176,1024]{1,0:T(8,128)(2,1)}, f32[8,128]{1,0:T(8,128)}, bf16[2048,1024]{1,0:T(8,128)(2,1)}) custom-call(bf16[1024,2048]{1,0:T(8,128)(2,1)} %get-tuple-element.35.refs_0_, bf16[2048,1024]{1,0:T(8,128)(2,1)} %bitcast.26, bf16[2,2,2,2,176,1024]{5,4,3,2,1,0:T(8,128)(2,1)} %bitcast.23, ...), custom_call_target="tpu_custom_call" | custom-call | tf_op jit(solution)/shard_map/reduce_layer_2/pallas_call | solution.py:489
  250.1 17.8 %convolution_convert_fusion = bf16[2816,1024]{1,0:T(8,128)(2,1)} fusion(bf16[2816,2048]{1,0:T(8,128)(2,1)} %get-tuple-element.42, bf16[2048,1024]{1,0:T(8,128)(2,1)} %get-tuple-element.41.refs_1_), kind=kOutput, calls=%fused_computation | convolution fusion | flops 11814043648 | bytes 21495808 | tf_op jit(solution)/shard_map/dot_general | solution.py:16
  267.8 0.0 copy-start.7
  267.8 88.3 %reduce_layer_1.1 = (bf16[64,5632]{1,0:T(8,128)(2,1)}, bf16[176,1024]{1,0:T(8,128)(2,1)}, f32[8,128]{1,0:T(8,128)}) custom-call(bf16[1024,2048]{1,0:T(8,128)(2,1)} %get-tuple-element.40.refs_0_, bf16[2048,1024]{1,0:T(8,128)(2,1)} %get-tuple-element.41.refs_1_, bf16[2,2,2,2,176,1024]{5,4,3,2,1,0:T(8,128)(2,1)} %bitcast.24, ...), custom_call_target="tpu_custom_call" | custom-call | tf_op jit(solution)/shard_map/reduce_layer_1/pallas_call | solution.py:489
  356.1 0.0 copy-done.7
  356.1 1.3 add.3.sq
  357.4 128.0 %step_and_gather.1 = (bf16[2,2,2,2,2,64,2816]{6,5,4,3,2,1,0:T(8,128)(2,1)}, bf16[2,2,2,2,2,64,2816]{6,5,4,3,2,1,0:T(8,128)(2,1)}, bf16[2,2,2,2,2,176,1024]{6,5,4...) custom-call(f32[8,128]{1,0:T(8,128)} %add.3.sq, ...), custom_call_target="tpu_custom_call" | custom-call | tf_op jit(solution)/shard_map/step_and_gather/pallas_call | solution.py:148
  485.4 0.0 copy-start
  485.4 0.0 slice-start
  485.4 0.0 slice-start.1
  485.5 11.7 %copy.29 = bf16[2,1024,2816]{2,1,0:T(8,128)(2,1)} copy(bf16[2,1024,2816]{2,1,0:T(8,128)(2,1)} %bitcast.22) | data formatting | bytes 23068672
  497.1 0.0 copy-done
  497.1 0.0 slice-start.2
  497.1 5.8 %copy.30 = bf16[2,1024,2816]{2,1,0:T(8,128)(2,1)} copy(bf16[2,1024,2816]{2,1,0:T(8,128)(2,1)S(1)} %bitcast.21) | data formatting | bytes 23068672
  503.0 0.0 slice-done
  503.0 0.7 slice-done.1
  503.7 1.3 slice-done.2
  505.0 0.0 copy-start.6
  505.0 0.0 copy-start.5
  505.0 4.8 copy.31
  509.8 0.0 copy-done.6
  509.8 0.0 copy-start.4
  509.8 0.0 copy-start.3
  509.8 1.1 copy.32
  510.9 0.0 copy-done.5
  510.9 0.0 copy-start.2
  510.9 1.1 copy.33
  512.0 0.0 copy-done.4
  512.0 0.0 copy-start.1
  512.0 1.1 copy.34
  513.1 0.0 copy-done.3
  513.1 1.1 copy.35
  514.2 0.0 copy-done.2
  514.3 1.1 copy.36
  515.4 0.0 copy-done.1
  515.4 1.1 copy.37
  (1 shorter events, 0.0 us)
Async XLA Ops:
  267.8 88.3 %copy-start.7 = (f32[8,128]{1,0:T(8,128)S(1)}, f32[8,128]{1,0:T(8,128)}, u32[]{:S(2)}) copy-start(f32[8,128]{1,0:T(8,128)} %get-tuple-element.39) | copy-start | bytes 12292
  485.4 11.7 %copy-start = (bf16[2,2,2,2,2,64,2816]{6,5,4,3,2,1,0:T(8,128)(2,1)S(1)}, bf16[2,2,2,2,2,64,2816]{6,5,4,3,2,1,0:T(8,128)(2,1)}, u32[]{:S(2)}) copy-start(bf16[2,2,2,2,2,64,2816]{6,5,4,3,2,1,0:T(8,128)(2,1)} %get-tuple-element.51) | copy-start | bytes 34603012
  485.4 17.6 %slice-start = ((s8[11534336]{0:T(1024)(128)(4,1)}), s8[4194304]{0:T(1024)(128)(4,1)S(1)}, s32[]{:S(2)}) async-start(s8[11534336]{0:T(1024)(128)(4,1)} %bitcast.18), calls=%async_computation | async-start | bytes 8388608
  485.4 18.2 %slice-start.1 = ((s8[11534336]{0:T(1024)(128)(4,1)}), s8[4194304]{0:T(1024)(128)(4,1)S(1)}, s32[]{:S(2)}) async-start(s8[11534336]{0:T(1024)(128)(4,1)} %bitcast.18), calls=%async_computation.1 | async-start | bytes 8388608
  497.1 7.8 %slice-start.2 = ((s8[11534336]{0:T(1024)(128)(4,1)}), s8[3145728]{0:T(1024)(128)(4,1)S(1)}, s32[]{:S(2)}) async-start(s8[11534336]{0:T(1024)(128)(4,1)} %bitcast.18), calls=%async_computation.2 | async-start | bytes 6291456
  505.0 4.9 copy-start.6
  505.0 6.0 %copy-start.5 = (f32[2,64,2816]{2,1,0:T(8,128)S(1)}, f32[2,64,2816]{2,1,0:T(8,128)}, u32[]{:S(2)}) copy-start(f32[2,64,2816]{2,1,0:T(8,128)} %get-tuple-element.72) | copy-start | bytes 4325380
  509.8 2.2 copy-start.4
  509.8 3.3 copy-start.3
  510.9 3.3 copy-start.2
  512.0 3.3 copy-start.1

commit v6 on v5

--- a/solution.py
+++ b/solution.py
@@ -40,9 +40,17 @@
     core = me % 2
     units = [(i, l) for l in reversed(range(shapes[0][0])) for i in range(n_mat)]
 
-    loads = [pltpu.make_async_copy(w[i].at[l, me], own_w[i].at[l], in_sem.at[u]) for u, (i, l) in enumerate(units)]
-    for copy in loads:
-        copy.start()
+    loads = [
+        [
+            pltpu.make_async_copy(w[i].at[l, me], own_w[i].at[l], in_sem.at[u, 0]),
+            pltpu.make_async_copy(m[i].at[l], out_m[i].at[l], in_sem.at[u, 1]),
+            pltpu.make_async_copy(v[i].at[l], out_v[i].at[l], in_sem.at[u, 2]),
+        ]
+        for u, (i, l) in enumerate(units)
+    ]
+    for copies in loads:
+        for copy in copies:
+            copy.start()
     barrier = pltpu.get_barrier_semaphore()
     for k in range(1, 16):
         pl.semaphore_signal(barrier, inc=1, device_id={"dp": (me + k) % 16}, device_id_type=MESH)
@@ -97,11 +105,12 @@
 
     moved, kept, stores = [], [], []
     for u, (i, l) in enumerate(units):
-        loads[u].wait()
+        for copy in loads[u]:
+            copy.wait()
         g = dn[l][...] if i == 2 else gu[l][:, i * ff : (i + 1) * ff]
         clipped = g.astype(jnp.float32) * factor
-        mm = 0.9 * m[i][l] + 0.1 * clipped
-        vv = 0.95 * v[i][l] + 0.05 * clipped * clipped
+        mm = 0.9 * out_m[i][l] + 0.1 * clipped
+        vv = 0.95 * out_v[i][l] + 0.05 * clipped * clipped
         old = own_w[i][l].astype(jnp.float32)
         out_w[i][l] = (old - 0.02 * (mm * lax.rsqrt(vv + 1e-8) + 0.1 * old)).astype(jnp.bfloat16)
         out_m[i][l] = mm
@@ -149,7 +158,7 @@
         functools.partial(gather_kernel, shapes, count),
         out_shape=[jax.ShapeDtypeStruct((s[0], 2, 2, 2, 2) + s[1:], jnp.bfloat16) for s in shapes]
         + [jax.ShapeDtypeStruct(s, jnp.float32) for s in shapes] * 2,
-        in_specs=[vmem] * (1 + len(gu) + len(dn)) + [hbm] * 3 + [vmem] * 6,
+        in_specs=[vmem] * (1 + len(gu) + len(dn)) + [hbm] * 9,
         out_specs=[hbm] * 9,
         scratch_shapes=[pltpu.VMEM(s, jnp.bfloat16) for s in shapes] * 2
         + [pltpu.VMEM(s, jnp.float32) for s in shapes] * 2
@@ -157,7 +166,7 @@
             pltpu.VMEM((16, 8, 128), jnp.float32),
             dma((16,)),
             dma((16,)),
-            dma((n_units,)),
+            dma((n_units, 3)),
             dma((n_units,)),
             dma((n_units, 2)),
             dma((3 * n_units, 3)),
@@ -171,9 +180,10 @@
     return [t.reshape(old.shape) for t, old in zip(out[:3], w)] + list(out[3:])
 
 
+PARTS = 2
 UNIT = 256
-LAGS = (2, 5, 8, 11)
-DOWN_STEPS = (3, 9, 14, 18)
+LAGS = (2, 7, 12, 17)
+DOWN_STEPS = (3, 11, 17, 22)
 
 
 def forward_kernel(last, h, w_gate, w_up, *refs):
@@ -181,10 +191,10 @@
         gate, up, z_t, a_t, a = refs
     else:
         w_down, gate, up, z_t, a_t, new_h, a, total = refs
-    j, part = pl.program_id(0), h.shape[0] // 4
+    j, part = pl.program_id(0), h.shape[0] // PARTS
 
     def over_parts(body):
-        lax.fori_loop(0, 4, lambda p, _: body(pl.ds(pl.multiple_of(p * part, part), part)), None)
+        lax.fori_loop(0, PARTS, lambda p, _: body(pl.ds(pl.multiple_of(p * part, part), part)), None)
 
     @pl.when(j == 0)
     def _():
@@ -203,7 +213,7 @@
         u = jnp.dot(a[rows], w_up[...], preferred_element_type=jnp.float32)
         gate[rows] = g
         up[rows] = u
-        z = (jax.nn.silu(g) * u).astype(jnp.bfloat16)
+        z = (g * logistic(g) * u).astype(jnp.bfloat16)
         z_t[:, rows] = z.T
         if not last:
             total[rows] += jnp.dot(z, w_down[...], preferred_element_type=jnp.float32)
@@ -242,13 +252,17 @@
     )(h, w_gate, w_up, *(() if last else (w_down,)))
 
 
+def logistic(g):
+    return 0.5 * jnp.tanh(0.5 * g) + 0.5
+
+
 def fold(t):
     t = jnp.sum(jnp.square(t).reshape(-1, 8, t.shape[-1]), axis=0)
     return sum(t[:, j : j + 128] for j in range(0, t.shape[-1], 128))
 
 
 def reduce_kernel(per, l, with_da, *refs):
-    a_t, d, down, gate, up, w_down, *refs = refs
+    a_t_hbm, d_hbm, down, gate, up, w_down, *refs = refs
     if with_da:
         w_gate, w_up, h, *refs = refs
     gu, dn, sq, *refs = refs
@@ -256,7 +270,7 @@
         new_d, *refs = refs
     tile, got, kept1, kept2, kept3, out1, out2, out3, in1, in2, in3 = refs[:11]
     d_own, d_got, d_kept1, d_kept2, d_kept3, d_out1, d_out2, d_out3, d_in1, d_in2, d_in3 = refs[11:22]
-    gates, ups, d_gu, wd, p_sem, w_sem, send, recv, d_send, d_recv, own_sem, *refs = refs[22:]
+    a_t, d, gates, ups, d_gu, wd, p_sem, w_sem, send, recv, d_send, d_recv, own_sem, whole_sem, *refs = refs[22:]
     if with_da:
         da, wgu, h_part, h_sem = refs
     kept, outs, ins = (kept1, kept2, kept3), (out1, out2, out3), (in1, in2, in3)
@@ -275,7 +289,7 @@
     def hop(u, k, stage):
         if stage == 0:
             return remote(tile.at[u % 3, :, :, :, 1 - core], got.at[u % 4], send.at[0, u], recv.at[0, u], 1)
-        return remote(outs[stage - 1].at[u], ins[stage - 1].at[u % 6], send.at[stage, u], recv.at[stage, u], LINKS[(k + stage - 1) % 3])
+        return remote(outs[stage - 1].at[u % 6], ins[stage - 1].at[u % 12], send.at[stage, u], recv.at[stage, u], LINKS[(k + stage - 1) % 3])
 
     def down_hop(k, stage):
         cols = pl.ds(*widths(dn.shape[1], 0)[k])
@@ -301,7 +315,7 @@
             if stage == 1:
                 mine, other = tile[(u % 3, *where, core)], got[(u % 4, *where)]
             else:
-                mine, other = kept[stage - 2][(u % 4, *where)], ins[stage - 2][(u % 6, *where)]
+                mine, other = kept[stage - 2][(u % 6, *where)], ins[stage - 2][(u % 12, *where)]
             return mine.astype(jnp.float32) + other.astype(jnp.float32)
 
         if stage == 4:
@@ -310,9 +324,14 @@
             sq[...] += fold(g.astype(jnp.float32))
             return
         away, here = halves(k, stage)
-        outs[stage - 1][u] = total(away).astype(jnp.bfloat16)
+
+        @pl.when(u >= 6)
+        def _():
+            hop(u - 6, k, stage).wait_send()
+
+        outs[stage - 1][u % 6] = total(away).astype(jnp.bfloat16)
         hop(u, k, stage).start()
-        kept[stage - 1][u % 4] = total(here)
+        kept[stage - 1][u % 6] = total(here)
 
     def add_down(k, stage):
         down_hop(k, stage - 1).wait_recv()
@@ -371,9 +390,10 @@
             dz = lax.dot_general(d[rows], wd[slot], (((1,), (1,)), ((), ())), preferred_element_type=jnp.float32)
             dz = dz.astype(jnp.bfloat16).astype(jnp.float32)
             g, u = gates[p], ups[p]
-            sig = jax.nn.sigmoid(g)
-            d_u = (dz * (g * sig)).astype(jnp.bfloat16)
-            d_g = (dz * u * (sig * (1 + g * (1 - sig)))).astype(jnp.bfloat16)
+            sig = logistic(g)
+            silu = g * sig
+            d_u = (dz * silu).astype(jnp.bfloat16)
+            d_g = (dz * u * (sig + silu * (1 - sig))).astype(jnp.bfloat16)
             d_gu[0, rows] = d_g
             d_gu[1, rows] = d_u
             if with_da:
@@ -387,17 +407,21 @@
 
         lax.fori_loop(0, parts, one, None)
 
+    if with_da:
+        block = h_part.shape[1]
+        blocks = d.shape[0] // block
+
     def h_load(p):
-        rows = pl.ds(pl.multiple_of(p * part, part), part)
+        rows = pl.ds(pl.multiple_of(p * block, block), block)
         return pltpu.make_async_copy(h.at[rows], h_part.at[p % 2], h_sem.at[0, p % 2])
 
     def d_store(p):
-        rows = pl.ds(pl.multiple_of(p * part, part), part)
+        rows = pl.ds(pl.multiple_of(p * block, block), block)
         return pltpu.make_async_copy(h_part.at[p % 2], new_d.at[rows], h_sem.at[1, p % 2])
 
     def norm_back(p):
         h_load(p).wait()
-        rows = pl.ds(pl.multiple_of(p * part, part), part)
+        rows = pl.ds(pl.multiple_of(p * block, block), block)
         wide = h_part[p % 2].astype(jnp.float32)
         scale = lax.rsqrt(jnp.mean(wide * wide, -1, keepdims=True) + 1e-6)
         grad = da[rows]
@@ -406,16 +430,19 @@
         h_part[p % 2] = total.astype(jnp.bfloat16)
         d_store(p).start()
 
-        @pl.when(p + 2 < parts)
+        @pl.when(p + 2 < blocks)
         def _():
             d_store(p).wait()
             h_load(p + 2).start()
 
     own = pltpu.make_async_copy(down.at[:, :, :, core], d_own, own_sem)
-    own.start()
+    wholes = [pltpu.make_async_copy(s, t, whole_sem.at[i]) for i, (s, t) in enumerate(((d_hbm, d), (a_t_hbm, a_t)))]
+    wholes[0].start()
     start(weight_loads(0))
     for p in range(parts):
         start(part_loads(0, p))
+    own.start()
+    wholes[1].start()
     barrier = pltpu.get_barrier_semaphore()
     for stride in (1, *LINKS):
         pl.semaphore_signal(barrier, inc=1, device_id={"dp": flipped(me, stride)}, device_id_type=MESH)
@@ -426,6 +453,8 @@
     if with_da:
         da[...] = jnp.zeros_like(da)
     own.wait()
+    for copy in wholes:
+        copy.wait()
 
     def step(t, _):
         for stage, lag in reversed(list(enumerate(LAGS, 1))):
@@ -460,7 +489,7 @@
                 for p in range(2):
                     h_load(p).start()
 
-            @pl.when((t >= n_units) & (t < n_units + parts))
+            @pl.when((t >= n_units) & (t < n_units + blocks))
             def _():
                 norm_back(t - n_units)
 
@@ -470,12 +499,12 @@
         for stage in (1, 2, 3):
             hop(u, 0, stage).wait_send()
 
-    lax.fori_loop(0, n_units, drain, None)
+    lax.fori_loop(n_units - 6, n_units, drain, None)
     for k in range(3):
         for stage in range(4):
             down_hop(k, stage).wait_send()
     if with_da:
-        for p in (parts - 2, parts - 1):
+        for p in (blocks - 2, blocks - 1):
             d_store(p).wait()
 
 
@@ -483,7 +512,7 @@
     width, tokens = a_t.shape
     ff = gate.shape[1]
     per, rows, d_rows, with_da = ff // UNIT, width // 16, ff // 16, weights is not None
-    n_units, part = 2 * per, tokens // 4
+    n_units, part = 2 * per, tokens // PARTS
     vmem, hbm = pl.BlockSpec(memory_space=pltpu.VMEM), pl.BlockSpec(memory_space=pl.ANY)
     dma, b16, f32 = pltpu.SemaphoreType.DMA, jnp.bfloat16, jnp.float32
     return pl.pallas_call(
@@ -494,35 +523,37 @@
             jax.ShapeDtypeStruct((8, 128), f32),
         ]
         + [jax.ShapeDtypeStruct((tokens, width), b16)] * with_da,
-        in_specs=[vmem] * 2 + [hbm] * (7 if with_da else 4),
+        in_specs=[hbm] * (9 if with_da else 6),
         out_specs=[vmem] * 3 + [hbm] * with_da,
         scratch_shapes=[
             pltpu.VMEM((3, 2, 2, 2, 2, rows, UNIT), b16),
             pltpu.VMEM((4, 2, 2, 2, rows, UNIT), b16),
-            pltpu.VMEM((4, 2, 2, rows, UNIT), f32),
-            pltpu.VMEM((4, 2, rows, UNIT), f32),
-            pltpu.VMEM((4, rows, UNIT), f32),
+            pltpu.VMEM((6, 2, 2, rows, UNIT), f32),
+            pltpu.VMEM((6, 2, rows, UNIT), f32),
+            pltpu.VMEM((6, rows, UNIT), f32),
         ]
-        + [pltpu.VMEM((slots, *lead, rows, UNIT), b16) for slots in (n_units, 6) for lead in ((2, 2), (2,), ())]
+        + [pltpu.VMEM((slots, *lead, rows, UNIT), b16) for slots in (6, 12) for lead in ((2, 2), (2,), ())]
         + [pltpu.VMEM((2, 2, 2, d_rows, width), b16)] * 2
         + [pltpu.VMEM((2, 2, d_rows, width), f32), pltpu.VMEM((2, d_rows, width), f32), pltpu.VMEM((d_rows, width), f32)]
         + [pltpu.VMEM((2, 2, d_rows, width), b16), pltpu.VMEM((2, d_rows, width), b16), pltpu.VMEM((d_rows, width), b16)] * 2
-        + [pltpu.VMEM((4, part, UNIT), f32)] * 2
+        + [pltpu.VMEM((width, tokens), b16), pltpu.VMEM((tokens, width), b16)]
+        + [pltpu.VMEM((PARTS, part, UNIT), f32)] * 2
         + [
             pltpu.VMEM((2, tokens, UNIT), b16),
             pltpu.VMEM((2, UNIT, width), b16),
-            dma((2, 4)),
+            dma((2, PARTS)),
             dma((3, 2)),
             dma((4, n_units)),
             dma((4, n_units)),
             dma((4, 3)),
             dma((4, 3)),
             dma(()),
+            dma((2,)),
         ]
         + [
             pltpu.VMEM((tokens, width), f32),
             pltpu.VMEM((2, 2, width, UNIT), b16),
-            pltpu.VMEM((2, part, width), b16),
+            pltpu.VMEM((2, tokens // 8, width), b16),
             dma((2, 2)),
         ]
         * with_da,

time: 517 us -> 491 us (0.950)
  Pallas kernels: 448 us -> 422 us
    pallas_call x2, Pallas kernels: 221 us -> 207 us  [reduce_layer(): pl.pallas_call(functools.partial(reduce_kernel, per, l, with_da), out_sha...]
    pallas_call x2, Pallas kernels: 99.1 us -> 90.5 us  [forward_layer(): pl.pallas_call(functools.partial(forward_kernel, last), grid=(ff // UNIT,...]
where the time goes in v6:
time: 491 us
  Pallas kernels  422 us (86%)
  matrix products  35.5 us (7%)
  local copies, waits for them, and re-layouts  31 us (6%)
    pallas_call x2, Pallas kernels, reduce_layer(): pl.pallas_call(functools.partial(reduce_kernel, per, l, with_da), out_sha...  207 us
    pallas_call x1, Pallas kernels, step_and_gather(): pl.pallas_call(functools.partial(gather_kernel, shapes, count), out_shape...  125 us
    pallas_call x2, Pallas kernels, forward_layer(): pl.pallas_call(functools.partial(forward_kernel, last), grid=(ff // UNIT,...  90.5 us
    dot_general x2, matrix products, dot(): lax.dot_general(a, b, (dims, ((), ())), preferred_element_type=jnp.float32)  35.5 us
    unnamed x31, local copies, waits for them, and re-layouts  31 us

profile of v6, /device:TPU:0, one launch (start us, length us, event | category | flops | bytes accessed | tf_op | source)
XLA Modules:
  0.0 490.9 jit_solution(10014389538044863599)
XLA Ops:
  0.6 52.4 %forward_layer_0.1 = (f32[2048,2816]{1,0:T(8,128)}, f32[2048,2816]{1,0:T(8,128)}, bf16[2816,2048]{1,0:T(8,128)(2,1)}, bf16[1024,2048]{1,0:T(8,128)(2,1)}, bf16[2048,1024]{1,0:T(8,128)(2,1)}) custom-call(bf16[2048,1024]{1,0:T(8,128)(2,1)} %bitcast.25, bf16[2,1024,2816]{2,1,0:T(8,128)(2,1)} %refs_6_.1, bf16[2,1024,2816]{2,1,0:T(8,128)(2,1)} %refs_7_.2, ...), custom_call_target="tpu_custom_call" | custom-call | tf_op jit(solution)/shard_map/forward_layer_0/pallas_call | solution.py:239
  53.1 38.0 %forward_layer_1.1 = (f32[2048,2816]{1,0:T(8,128)}, f32[2048,2816]{1,0:T(8,128)}, bf16[2816,2048]{1,0:T(8,128)(2,1)}, bf16[1024,2048]{1,0:T(8,128)(2,1)}) custom-call(bf16[2048,1024]{1,0:T(8,128)(2,1)} %get-tuple-element.34.h.refs_8_, bf16[2,1024,2816]{2,1,0:T(8,128)(2,1)} %refs_6_.1, bf16[2,1024,2816]{2,1,0:T(8,128)(2,1)} %refs_7_.2), custom_call_target="tpu_custom_call" | custom-call | tf_op jit(solution)/shard_map/forward_layer_1/pallas_call | solution.py:239
  91.1 17.8 %convolution_convert_fusion.1 = bf16[2816,1024]{1,0:T(8,128)(2,1)} fusion(bf16[2816,2048]{1,0:T(8,128)(2,1)} %get-tuple-element.36, bf16[1,2048,1024]{2,1,0:T(8,128)(2,1)} %param.12), kind=kOutput, calls=%fused_computation.1 | convolution fusion | flops 11814043648 | bytes 21495808 | tf_op jit(solution)/shard_map/dot_general | solution.py:16
  108.9 126.7 %reduce_layer_2.1 = (bf16[64,5632]{1,0:T(8,128)(2,1)}, bf16[176,1024]{1,0:T(8,128)(2,1)}, f32[8,128]{1,0:T(8,128)}, bf16[2048,1024]{1,0:T(8,128)(2,1)}) custom-call(bf16[1024,2048]{1,0:T(8,128)(2,1)} %get-tuple-element.35.refs_0_, bf16[2048,1024]{1,0:T(8,128)(2,1)} %bitcast.26, bf16[2,2,2,2,176,1024]{5,4,3,2,1,0:T(8,128)(2,1)} %bitcast.23, ...), custom_call_target="tpu_custom_call" | custom-call | tf_op jit(solution)/shard_map/reduce_layer_2/pallas_call | solution.py:518
  235.6 17.8 %convolution_convert_fusion = bf16[2816,1024]{1,0:T(8,128)(2,1)} fusion(bf16[2816,2048]{1,0:T(8,128)(2,1)} %get-tuple-element.42, bf16[2048,1024]{1,0:T(8,128)(2,1)} %get-tuple-element.41.refs_1_), kind=kOutput, calls=%fused_computation | convolution fusion | flops 11814043648 | bytes 21495808 | tf_op jit(solution)/shard_map/dot_general | solution.py:16
  253.4 0.0 copy-start.7
  253.4 80.4 %reduce_layer_1.1 = (bf16[64,5632]{1,0:T(8,128)(2,1)}, bf16[176,1024]{1,0:T(8,128)(2,1)}, f32[8,128]{1,0:T(8,128)}) custom-call(bf16[1024,2048]{1,0:T(8,128)(2,1)} %get-tuple-element.40.refs_0_, bf16[2048,1024]{1,0:T(8,128)(2,1)} %get-tuple-element.41.refs_1_, bf16[2,2,2,2,176,1024]{5,4,3,2,1,0:T(8,128)(2,1)} %bitcast.24, ...), custom_call_target="tpu_custom_call" | custom-call | tf_op jit(solution)/shard_map/reduce_layer_1/pallas_call | solution.py:518
  333.7 0.0 copy-done.7
  333.7 1.3 add.3.sq
  335.0 124.8 %step_and_gather.1 = (bf16[2,2,2,2,2,64,2816]{6,5,4,3,2,1,0:T(8,128)(2,1)}, bf16[2,2,2,2,2,64,2816]{6,5,4,3,2,1,0:T(8,128)(2,1)}, bf16[2,2,2,2,2,176,1024]{6,5,4...) custom-call(f32[8,128]{1,0:T(8,128)} %add.3.sq, ...), custom_call_target="tpu_custom_call" | custom-call | tf_op jit(solution)/shard_map/step_and_gather/pallas_call | solution.py:157
  459.8 0.0 copy-start
  459.8 0.0 slice-start
  459.8 0.0 slice-start.1
  459.9 11.7 %copy.29 = bf16[2,1024,2816]{2,1,0:T(8,128)(2,1)} copy(bf16[2,1024,2816]{2,1,0:T(8,128)(2,1)} %bitcast.22) | data formatting | bytes 23068672
  471.5 0.0 copy-done
  471.5 0.0 slice-start.2
  471.5 5.8 %copy.30 = bf16[2,1024,2816]{2,1,0:T(8,128)(2,1)} copy(bf16[2,1024,2816]{2,1,0:T(8,128)(2,1)S(1)} %bitcast.21) | data formatting | bytes 23068672
  477.4 0.0 slice-done
  477.4 0.7 slice-done.1
  478.1 1.3 slice-done.2
  479.4 0.0 copy-start.6
  479.4 0.0 copy-start.5
  479.4 4.8 copy.31
  484.2 0.0 copy-done.6
  484.2 0.0 copy-start.4
  484.2 0.0 copy-start.3
  484.2 1.1 copy.32
  485.3 0.0 copy-done.5
  485.3 0.0 copy-start.2
  485.3 1.1 copy.33
  486.4 0.0 copy-done.4
  486.5 0.0 copy-start.1
  486.5 1.1 copy.34
  487.6 0.0 copy-done.3
  487.6 1.1 copy.35
  488.7 0.0 copy-done.2
  488.7 1.1 copy.36
  489.8 0.0 copy-done.1
  489.8 1.1 copy.37
  (1 shorter events, 0.0 us)
Async XLA Ops:
  253.4 80.4 %copy-start.7 = (f32[8,128]{1,0:T(8,128)S(1)}, f32[8,128]{1,0:T(8,128)}, u32[]{:S(2)}) copy-start(f32[8,128]{1,0:T(8,128)} %get-tuple-element.39) | copy-start | bytes 12292
  459.8 11.7 %copy-start = (bf16[2,2,2,2,2,64,2816]{6,5,4,3,2,1,0:T(8,128)(2,1)S(1)}, bf16[2,2,2,2,2,64,2816]{6,5,4,3,2,1,0:T(8,128)(2,1)}, u32[]{:S(2)}) copy-start(bf16[2,2,2,2,2,64,2816]{6,5,4,3,2,1,0:T(8,128)(2,1)} %get-tuple-element.51) | copy-start | bytes 34603012
  459.8 17.6 %slice-start = ((s8[11534336]{0:T(1024)(128)(4,1)}), s8[4194304]{0:T(1024)(128)(4,1)S(1)}, s32[]{:S(2)}) async-start(s8[11534336]{0:T(1024)(128)(4,1)} %bitcast.18), calls=%async_computation | async-start | bytes 8388608
  459.8 18.2 %slice-start.1 = ((s8[11534336]{0:T(1024)(128)(4,1)}), s8[4194304]{0:T(1024)(128)(4,1)S(1)}, s32[]{:S(2)}) async-start(s8[11534336]{0:T(1024)(128)(4,1)} %bitcast.18), calls=%async_computation.1 | async-start | bytes 8388608
  471.5 7.8 %slice-start.2 = ((s8[11534336]{0:T(1024)(128)(4,1)}), s8[3145728]{0:T(1024)(128)(4,1)S(1)}, s32[]{:S(2)}) async-start(s8[11534336]{0:T(1024)(128)(4,1)} %bitcast.18), calls=%async_computation.2 | async-start | bytes 6291456
  479.4 4.9 copy-start.6
  479.4 6.0 %copy-start.5 = (f32[2,64,2816]{2,1,0:T(8,128)S(1)}, f32[2,64,2816]{2,1,0:T(8,128)}, u32[]{:S(2)}) copy-start(f32[2,64,2816]{2,1,0:T(8,128)} %get-tuple-element.72) | copy-start | bytes 4325380
  484.2 2.2 copy-start.4
  484.2 3.3 copy-start.3
  485.3 3.3 copy-start.2
  486.5 3.3 copy-start.1
